TPU v7x, 128 devices: a whole 4x4x4 slice. The times are simulated.
128 devices in a mesh: seq: 16 (over x_lo, y, core), hid: 8 (over x_hi, z).
Axes of the slice: x: 4 (x_hi: 2, x_lo: 2; x = x_hi * 2 + x_lo), y: 4, z: 4, core: 2. Of those that a mesh axis runs over, the one named last changes fastest.
Arguments:
- hidden: bfloat16 [8192, 4096], P('seq', 'hid'), may hold values from -6 to 6
- w_in: bfloat16 [2, 4096, 1024], P(None, 'hid'), may hold values from -0.09863281 to 0.09863281
- embedding: bfloat16 [1, 2048, 1024], replicated, may hold values from -6 to 6
- depth_gain: float32 [2, 1024], replicated, may hold values from 0.25 to 1.75
- w_out: bfloat16 [1024, 2, 2048], P(('seq', 'hid')), may hold values from -0.43554688 to 0.43554688
- codebook_ids: int32 [2, 8192], P(None, ('seq', 'hid')), may hold values from 0 to 2047
Outputs:
- grad_hidden: bfloat16 [8192, 4096], P('seq', 'hid')
- grad_in: float32 [2, 4096, 1024], P(None, 'hid', 'seq')
- grad_out: float32 [1024, 2, 2048], P(('seq', 'hid'))
All inputs are finite; a program needn't handle non-finite values.
Results may differ from a plain program's by a relative error of at most 0.01.
Values may be sent and summed in bfloat16 or wider, within the bound.
A program may use at most 128 MiB of HBM per device.

v0:
```python
import jax
import jax.numpy as jnp
from jax import lax
from jax.sharding import PartitionSpec as P


def shards(hidden, w_in, embedding, depth_gain, w_out, codebook_ids):
    hid_count = lax.axis_size("hid")
    seq_count = lax.axis_size("seq")
    width_in = hidden.shape[1] * hid_count
    steps = w_in.shape[0]
    depth = w_in.shape[2]
    entries = w_out.shape[2]
    group_rows = hidden.shape[0]
    hidden_f = hidden.astype(jnp.float32)
    square_part = jnp.sum(hidden_f * hidden_f, axis=1)
    proj_part = jnp.einsum("fd,kde->fke", hidden, w_in, preferred_element_type=jnp.float32)
    proj_flat, squares = (
        lax.psum_scatter(
            proj_part.reshape(group_rows, steps * depth), "hid", scatter_dimension=0, tiled=True
        ),
        lax.psum_scatter(square_part, "hid", scatter_dimension=0, tiled=True),
    )
    owned = proj_flat.shape[0]
    proj = proj_flat.reshape(owned, steps, depth)
    ratio = lax.rsqrt(squares / width_in + 1e-06)
    pieces = [jnp.zeros((owned, depth), jnp.float32)]
    pieces.append(jnp.take(embedding[0], codebook_ids[0], axis=0).astype(jnp.float32))
    x_rows = ratio[:, None, None] * proj + jnp.stack(pieces, axis=1)
    scale = lax.rsqrt(jnp.mean(x_rows * x_rows, axis=2, keepdims=True) + 1e-06)
    normed = (x_rows * scale * depth_gain[None]).astype(jnp.bfloat16)
    full_head = lax.all_gather(w_out, ("seq", "hid"), axis=0, tiled=True)
    logits = jnp.einsum("fkd,dkc->fkc", normed, full_head, preferred_element_type=jnp.float32)
    targets = codebook_ids.T
    lse = jax.nn.logsumexp(logits, axis=2)
    onehot = (targets[:, :, None] == jnp.arange(entries, dtype=jnp.int32)[None, None, :]).astype(
        jnp.float32
    )
    loss_weight = 2.0 * entries / (owned * seq_count * hid_count)
    d_logit = ((jnp.exp(logits - lse[:, :, None]) - onehot) * loss_weight).astype(jnp.bfloat16)
    grad_out = lax.psum_scatter(
        jnp.einsum("fkd,fkc->dkc", normed, d_logit, preferred_element_type=jnp.float32),
        ("seq", "hid"),
        scatter_dimension=0,
        tiled=True,
    )
    d_norm = jnp.einsum("fkc,dkc->fkd", d_logit, full_head, preferred_element_type=jnp.float32)
    gated = depth_gain[None] * d_norm
    d_x = scale * gated - x_rows * scale**3 * jnp.mean(gated * x_rows, axis=2, keepdims=True)
    d_round = d_x.astype(jnp.bfloat16)
    d_ratio = jnp.sum(d_x * proj, axis=(1, 2))
    correction = ratio**3 * d_ratio / width_in
    rows_back, ratio_back, corr_back = (
        lax.all_gather(d_round, "hid", axis=0, tiled=True),
        lax.all_gather(ratio.astype(jnp.bfloat16), "hid", axis=0, tiled=True).astype(ratio.dtype),
        lax.all_gather(correction.astype(jnp.bfloat16), "hid", axis=0, tiled=True).astype(
            correction.dtype
        ),
    )
    scaled = (ratio_back[:, None, None] * rows_back.astype(jnp.float32)).astype(jnp.bfloat16)
    in_term = jnp.einsum("fd,fke->kde", hidden, scaled, preferred_element_type=jnp.float32)
    grad_in = lax.psum_scatter(in_term, "seq", scatter_dimension=2, tiled=True)
    back = jnp.einsum("fke,kde->fd", rows_back, w_in, preferred_element_type=jnp.float32)
    grad_hidden = (ratio_back[:, None] * back - corr_back[:, None] * hidden_f).astype(jnp.bfloat16)
    return (grad_hidden, grad_in, grad_out)


def solution(mesh):
    placed = (
        P("seq", "hid"),
        P(None, "hid", None),
        P(),
        P(),
        P(("seq", "hid"), None, None),
        P(None, ("seq", "hid")),
    )
    return jax.shard_map(
        shards,
        mesh=mesh,
        in_specs=placed,
        out_specs=(P("seq", "hid"), P(None, "hid", "seq"), P(("seq", "hid"), None, None)),
        check_vma=False,
    )
```

profile of v0, /device:TPU:0, one launch (start us, length us, event | category | flops | bytes accessed | tf_op | source)
XLA Modules:
  0.0 623.3 jit_solution(17267702258610093383)
XLA Ops:
  8.1 1.5 copy-done
  9.6 4.3 fusion.7
  13.9 5.4 copy.31
  19.3 0.0 all-gather.3.cloned.1.call-start
  19.4 0.7 copy-done.5
  20.1 0.7 copy.22
  20.9 0.6 fusion.16
  22.2 3.5 gather_fusion
  25.7 0.2 fusion.5
  25.9 26.2 %all-reduce.3 = f32[512]{0:T(512)S(1)} all-reduce(f32[512]{0:T(512)S(1)} %fusion.5), channel_id=2, replica_groups=mesh['seq'=16,'hid'=8] {'hid'}, use_global_device_ids=true, to_apply=%region_1.0.clone | all-reduce | flops 512 | bytes 4096
  52.1 0.1 fusion.14
  52.2 0.1 bitcast_select_fusion
  52.3 55.9 %reduce-scatter.7.cloned.1.call-done = f32[64,2048]{1,0:T(8,128)} async-done(((f32[512,2048]{1,0:T(8,128)}), f32[64,2048]{1,0:T(8,128)}) %reduce-scatter.7.cloned.1.call-update) | async-done | bytes 524304
  108.2 2.4 copy.32
  110.7 1.5 copy.21
  112.2 0.2 multiply_reduce_fusion.2
  112.4 233.5 %all-gather.3.cloned.1.call-done = bf16[1024,2,2048]{2,0,1:T(8,128)(2,1)} async-done(((bf16[8,2,2048]{2,0,1:T(8,128)(2,1)}), bf16[1024,2,2048]{2,0,1:T(8,128)(2,1)}) %all-gather.3.cloned.1.call-update) | async-done | bytes 8388624 | tf_op jit(solution)/shard_map/all_gather | solution.py:32
  345.9 5.3 fusion.17
  351.2 0.3 exponential_reduce_fusion
  351.5 0.2 copy-done.1
  351.7 2.8 multiply_reduce_fusion.1
  354.5 1.0 multiply_reduce_fusion
  355.5 0.0 all-reduce.8.cloned.1.call-start
  355.6 9.4 %convolution_bitcast_fusion = f32[1024,2,2048]{0,2,1:T(8,128)} fusion(f32[2,1024]{1,0:T(2,128)S(1)} %copy-done.4, f32[64,2]{0,1:T(2,128)S(1)} %get-tuple-element.16, f32[64,2,2048]{2,0,1:T(8,128)} %copy-done.2, s32[64,2]{0,1:T(2,128)S(1)} %bitcast.45, f32[64,2]{0,1:T(2,128)S(1)} %log_add_fusion, f32[64,2,1024]{2,0,1:T(8,128)S(1)} %copy.21, ...), kind=kOutput, calls=%fused_computation.1 | convolution fusion | flops 539230208 | bytes 18491136 | tf_op jit(solution)/shard_map/fkd,fkc->dkc/dot_general | solution.py:42
  365.0 25.4 %copy.25 = f32[1024,2,2048]{2,1,0:T(2,128)} copy(f32[1024,2,2048]{0,2,1:T(8,128)} %convolution_bitcast_fusion) | data formatting | bytes 33554432 | tf_op jit(solution)/shard_map/fkd,fkc->dkc/transpose | solution.py:42
  391.2 0.2 dynamic-update-slice
  391.4 0.2 dynamic-update-slice.1
  391.7 26.4 %all-reduce.5 = (bf16[512]{0:T(512)(128)(2,1)S(1)}, bf16[512]{0:T(512)(128)(2,1)S(1)}) all-reduce(bf16[512]{0:T(512)(128)(2,1)S(1)} %dynamic-update-slice.1, bf16[512]{0:T(512)(128)(2,1)S(1)} %dynamic-update-slice), channel_id=1, replica_groups=mesh['seq'=16,'hid'=8] {'hid'}, use_global_device_ids=true, to_apply=%add.2 | all-reduce | flops 1024 | bytes 4096
  418.1 5.2 convolution_bitcast_fusion.2
  423.3 3.8 fusion.3
  427.1 187.6 %all-reduce.8.cloned.1.call-done = f32[1024,2,2048]{2,1,0:T(2,128)} async-done(((f32[1024,2,2048]{2,1,0:T(2,128)}), f32[1024,2,2048]{2,1,0:T(2,128)}) %all-reduce.8.cloned.1.call-update) | async-done | bytes 16777232
  614.7 1.6 constant_dynamic-slice_fusion
  (35 shorter events, 0.3 us)
Async XLA Ops:
  8.0 1.6 copy-start
  8.0 100.2 %reduce-scatter.7.cloned.1.call-start = ((), (), s32[]{:S(2)}) async-start(), calls=%async_computation.5 | async-start | bytes 4718592
  19.3 0.8 copy-start.5
  19.3 1.6 copy-start.7
  19.3 2.8 copy-start.6
  19.3 6.4 %copy-start.3 = (bf16[512,512]{1,0:T(8,128)(2,1)S(1)}, bf16[512,512]{1,0:T(8,128)(2,1)}, u32[]{:S(2)}) copy-start(bf16[512,512]{1,0:T(8,128)(2,1)} %param.6) | copy-start | bytes 1572868
  19.3 326.6 %copy-start.4 = (f32[2,1024]{1,0:T(2,128)S(1)}, f32[2,1024]{1,0:T(2,128)}, u32[]{:S(2)}) copy-start(f32[2,1024]{1,0:T(2,128)} %param.9) | copy-start | bytes 24580
  19.3 326.6 %all-gather.3.cloned.1.call-start = ((), (), s32[]{:S(2)}) async-start(), calls=%async_computation.2 | async-start | bytes 8454144 | tf_op jit(solution)/shard_map/all_gather | solution.py:32
  20.8 397.3 %all-gather.5.cloned.1.call-start = ((), (), s32[]{:S(2)}) async-start(), calls=%async_computation.3 | async-start | bytes 2359296 | tf_op jit(solution)/shard_map/all_gather | solution.py:54
  345.9 5.8 copy-start.1
  351.2 3.3 copy-start.2
  355.5 259.1 %all-reduce.8.cloned.1.call-start = ((), (), s32[]{:S(2)}) async-start(), calls=%async_computation.6 | async-start | bytes 33554432
  390.4 225.8 %reduce-scatter.5.cloned.1.call-start = ((), (), s32[]{:S(2)}) async-start(), calls=%async_computation.4 | async-start | bytes 4456448 | tf_op jit(solution)/shard_map/reduce_scatter | solution.py:62
Sparse Core Ops, SparseCore 0:
  19.5 88.7 reduce-scatter.6
  355.6 57.8 all-gather.4
  423.4 67.9 reduce-scatter.4
Sparse Core Ops, SparseCore 1:
  22.1 323.7 all-gather.2
  390.5 224.1 all-reduce.7
where the time goes:
time: 625 us; the launch traced here: 623 us
  waiting for transfers between devices  477 us (76%)
  blocking collectives  52.6 us (8%)
  local copies, waits for them, and re-layouts  44.2 us (7%)
  matrix products  30.7 us (5%)
  between operations  16.6 us (3%)
    unnamed x7, waiting for transfers between devices  244 us
    all_gather x1, waiting for transfers between devices, shards(): full_head = lax.all_gather(w_out, ('seq', 'hid'), axis=0, tiled=True)  233 us
    unnamed x2, blocking collectives  52.6 us
    transpose x1, local copies, waits for them, and re-layouts, shards(): jnp.einsum('fkd,fkc->dkc', normed, d_logit, preferred_element_type=jnp.fl...  25.4 us
    unnamed x25, local copies, waits for them, and re-layouts  13.7 us
  transfers between devices with their start and end apart: 5, of which 3 were waited for; matrix products, arithmetic and copies ran while one was open for 9% of the time, Pallas kernels for 0%

commit v1 on v0

v1 whole, which is shorter than its diff:
```python
import functools

import jax
import jax.numpy as jnp
from jax import lax
from jax.experimental import pallas as pl
from jax.experimental.pallas import tpu as pltpu
from jax.sharding import PartitionSpec as P

MESH = pl.DeviceIdType.MESH
BF = jnp.bfloat16
F32 = jnp.float32


def place():
    s, h = lax.axis_index("seq"), lax.axis_index("hid")
    x_lo, y, c = lax.div(s, 8), lax.rem(lax.div(s, 2), 4), lax.rem(s, 2)
    return 2 * lax.div(h, 4) + x_lo, y, lax.rem(h, 4), c


def device(x, y, z, c):
    x, y, z, c = lax.rem(x, 4), lax.rem(y, 4), lax.rem(z, 4), lax.rem(c, 2)
    return (lax.rem(x, 2) * 8 + y * 2 + c, lax.div(x, 2) * 4 + z)


def greet(peers):
    barrier = pltpu.get_barrier_semaphore()
    for peer in peers:
        pl.semaphore_signal(barrier, inc=1, device_id=peer, device_id_type=MESH)
    pl.semaphore_wait(barrier, len(peers))


class Post:
    def __init__(self, send_sem, recv_sem):
        self.send_sem, self.recv_sem, self.copies = send_sem, recv_sem, []

    def send(self, src, dst, peer):
        i = len(self.copies)
        copy = pltpu.make_async_remote_copy(
            src_ref=src,
            dst_ref=dst,
            send_sem=self.send_sem.at[i],
            recv_sem=self.recv_sem.at[i],
            device_id=peer,
            device_id_type=MESH,
        )
        copy.start()
        self.copies.append(copy)
        return copy

    def close(self):
        for copy in self.copies:
            copy.wait_send()


def forward_kernel(
    hidden, w_in, w_rows, ids, proj, sq_all, w_full, ids_all,
    part, got, w_pair, sq_mine, send_sem, recv_sem,
):
    x, y, z, c = place()
    x_lo, x_hi, step, zh = lax.rem(x, 2), lax.div(x, 2), lax.rem(z, 2), lax.div(z, 2)
    pair = device(x, y, z + 1 - 2 * step, c)
    across = device(x, y, z + 2, c)
    twin = device(x, y, z, c + 1)
    hid_peers = [(dx, dz) for dz in (2, 1, 3, 0) for dx in (2, 0) if (dx, dz) != (0, 0)]
    greet(
        [device(x + dx, y, z + dz, c) for dx, dz in hid_peers]
        + [device(x + d, y, z, c) for d in (1, 3)]
        + [device(x, y + d, z, c) for d in (1, 2, 3)]
        + [twin]
    )
    post = Post(send_sem, recv_sem)
    hid = x_hi * 4 + z

    w_swap = post.send(w_rows.at[1 - step], w_pair, pair)
    ids_swap = post.send(ids, ids_all.at[step], pair)
    ids_all[step] = ids[...]

    h = hidden[...].astype(F32)
    h2 = h * h
    top = h2.astype(BF)
    low = (h2 - top.astype(F32)).astype(BF)
    ones = jnp.ones((8, h2.shape[1]), BF)
    dims = (((1,), (1,)), ((), ()))
    sq_mine[...] = lax.dot_general(ones, top, dims, preferred_element_type=F32) + lax.dot_general(
        ones, low, dims, preferred_element_type=F32
    )
    sq_all[hid] = sq_mine[...]
    sq_copies = [
        post.send(sq_mine, sq_all.at[hid], device(x + dx, y, z + dz, c)) for dx, dz in hid_peers
    ]

    chunk_copies = []

    def chunk(dz):
        to_z = lax.rem(z + dz, 4)
        to_step, to_zh = lax.rem(to_z, 2), lax.div(to_z, 2)
        rows = [
            hidden[pl.ds(pl.multiple_of((fx * 2 + to_zh) * 128, 128), 128), :] for fx in range(2)
        ]
        product = jnp.dot(
            jnp.concatenate(rows, axis=0), w_in[to_step], preferred_element_type=F32
        ).astype(BF)
        part[dz, 0] = product[:128]
        part[dz, 1] = product[128:]
        for dx in (2, 0):
            if (dx, dz) == (0, 0):
                continue
            fx = 1 - x_hi if dx == 2 else x_hi
            slot = len(chunk_copies)
            chunk_copies.append(
                post.send(part.at[dz, fx], got.at[slot], device(x + dx, y, z + dz, c))
            )

    chunk(2)
    w_swap.wait_recv()
    mine = w_rows[step].astype(F32)
    other = w_pair[...].astype(F32)
    first = jnp.where(step == 0, mine, other)
    second = jnp.where(step == 0, other, mine)
    w_full[x_lo, y, c, x_hi, zh] = jnp.concatenate([first, second], axis=0).astype(BF)
    block = w_full.at[x_lo, y, c, x_hi, zh]
    w_across = post.send(block, block, across)
    w_x = [post.send(block, block, device(x + d, y, z, c)) for d in (1, 3, 2)]
    chunk(1)
    chunk(3)
    w_across.wait_recv()
    block = w_full.at[x_lo, y, c, x_hi, 1 - zh]
    w_x += [post.send(block, block, device(x + d, y, z, c)) for d in (1, 3, 2)]
    chunk(0)
    for copy in w_x:
        copy.wait_recv()
    line = w_full.at[:, y, c]
    w_y = [post.send(line, line, device(x, y + d, z, c)) for d in (2, 1, 3)]
    w_c = [post.send(line, line, twin)]

    for copy in chunk_copies:
        copy.wait_recv()
    total = part[0, x_hi].astype(F32)
    for slot in range(7):
        total = total + got[slot].astype(F32)
    proj[...] = total
    ids_swap.wait_recv()
    for copy in sq_copies:
        copy.wait_recv()

    for d, copy in zip((1, 3, 2), (w_y[1], w_y[2], w_y[0])):
        copy.wait_recv()
        line = w_full.at[:, lax.rem(y + 4 - d, 4), c]
        w_c.append(post.send(line, line, twin))
    for copy in w_c:
        copy.wait_recv()
    post.close()


def return_kernel(
    d_rows, small, partial, d_all, small_all, summed, c_got, y_out, y_got, send_sem, recv_sem
):
    x, y, z, c = place()
    x_hi, step, zh = lax.div(x, 2), lax.rem(z, 2), lax.div(z, 2)
    twin = device(x, y, z, c + 1)
    hid_peers = [(dx, dz) for dz in (2, 1, 3, 0) for dx in (2, 0) if (dx, dz) != (0, 0)]
    greet(
        [device(x + dx, y, z + dz, c) for dx, dz in hid_peers]
        + [device(x, y + d, z, c) for d in (1, 2, 3)]
        + [twin]
    )
    post = Post(send_sem, recv_sem)
    hid = x_hi * 4 + z
    c_swap = [
        post.send(
            partial.at[:, lax.rem(y + d, 4), 1 - c], c_got.at[:, lax.rem(y + d, 4)], twin
        )
        for d in (2, 1, 3, 0)
    ]
    rows_copies = []
    for dx, dz in hid_peers:
        peer = device(x + dx, y, z + dz, c)
        rows_copies.append(post.send(d_rows, d_all.at[step, x_hi, zh], peer))
        rows_copies.append(post.send(small, small_all.at[hid], peer))
    d_all[step, x_hi, zh] = d_rows[...]
    small_all[hid] = small[...]

    y_copies = []
    for i, d in enumerate((2, 1, 3)):
        c_swap[i].wait_recv()
        to_y = lax.rem(y + d, 4)

        @pl.loop(0, 8)
        def add(j):
            a, b, e = lax.div(j, 4), lax.rem(lax.div(j, 2), 2), lax.rem(j, 2)
            y_out[i, a, b, e] = (
                partial[a, to_y, c, b, e].astype(F32) + c_got[a, to_y, b, e].astype(F32)
            ).astype(BF)

        y_copies.append(post.send(y_out.at[i], y_got.at[i], device(x, y + d, z, c)))
    c_swap[3].wait_recv()
    for copy in rows_copies:
        copy.wait_recv()
    for copy in y_copies:
        copy.wait_recv()

    @pl.loop(0, 8)
    def total(j):
        a, b, e = lax.div(j, 4), lax.rem(lax.div(j, 2), 2), lax.rem(j, 2)
        value = partial[a, y, c, b, e].astype(F32) + c_got[a, y, b, e].astype(F32)
        for i in range(3):
            value = value + y_got[i, a, b, e].astype(F32)
        summed[a, b, e] = value.astype(BF)

    post.close()


def last_kernel(
    in_part, out_part, grad_in, grad_out,
    c_got, y_out, y_got, x_out, x_got, gx_got, z_out, z_got, rows, send_sem, recv_sem,
):
    x, y, z, c = place()
    x_lo, x_hi, step, zh = lax.rem(x, 2), lax.div(x, 2), lax.rem(z, 2), lax.div(z, 2)
    twin = device(x, y, z, c + 1)
    pair = device(x, y, z + 1 - 2 * step, c)
    across = device(x, y, z + 2, c)
    beside = device(x + 1 - 2 * x_lo, y, z, c)
    greet(
        [device(x + d, y, z, c) for d in (1, 2, 3)]
        + [device(x, y + d, z, c) for d in (1, 2, 3)]
        + [twin, pair, across]
    )
    post = Post(send_sem, recv_sem)
    c_swap = [
        post.send(
            in_part.at[:, :, lax.rem(y + d, 4), 1 - c], c_got.at[:, :, lax.rem(y + d, 4)], twin
        )
        for d in (2, 1, 3, 0)
    ]
    gx = []
    for i, d in enumerate((2, 1, 3)):
        to_x = lax.rem(x + d, 4)
        gx.append(
            post.send(
                out_part.at[lax.rem(to_x, 2), lax.div(to_x, 2)],
                gx_got.at[i],
                device(x + d, y, z, c),
            )
        )
    y_copies = []
    for i, d in enumerate((2, 1, 3)):
        c_swap[i].wait_recv()
        to_y = lax.rem(y + d, 4)

        @pl.loop(0, 4)
        def add(j):
            a, b = lax.div(j, 2), lax.rem(j, 2)
            y_out[i, a, b] = (
                in_part[a, b, to_y, c].astype(F32) + c_got[a, b, to_y].astype(F32)
            ).astype(BF)

        y_copies.append(post.send(y_out.at[i], y_got.at[i], device(x, y + d, z, c)))
    for copy in gx:
        copy.wait_recv()

    def block(e):
        value = out_part[x_lo, x_hi, e].astype(F32)
        for i in range(3):
            value = value + gx_got[i, e].astype(F32)
        return value

    z_out[...] = block(1 - zh).astype(BF)
    gz = post.send(z_out, z_got, across)
    c_swap[3].wait_recv()
    gz.wait_recv()
    rows[...] = block(zh) + z_got[...].astype(F32)
    theirs = rows.at[pl.ds(pl.multiple_of((1 - step) * 8, 8), 8), :]
    gp = post.send(theirs, grad_out.at[step], pair)
    grad_out[step] = rows[pl.ds(pl.multiple_of(step * 8, 8), 8), :]
    for copy in y_copies:
        copy.wait_recv()

    def line(a, b):
        value = in_part[a, b, y, c].astype(F32) + c_got[a, b, y].astype(F32)
        for i in range(3):
            value = value + y_got[i, a, b].astype(F32)
        return value

    for a in range(2):
        x_out[a] = line(a, 1 - x_lo).astype(BF)
    gi = post.send(x_out, x_got, beside)
    for a in range(2):
        grad_in[a] = line(a, x_lo)
    gi.wait_recv()
    for a in range(2):
        grad_in[a] = grad_in[a] + x_got[a].astype(F32)
    gp.wait_recv()
    post.close()


def call(kernel, index, outs, scratch, copies, *args):
    vmem = pl.BlockSpec(memory_space=pltpu.VMEM)
    return pl.pallas_call(
        kernel,
        out_shape=[jax.ShapeDtypeStruct(shape, dtype) for shape, dtype in outs],
        in_specs=[vmem] * len(args),
        out_specs=[vmem] * len(outs),
        scratch_shapes=[pltpu.VMEM(shape, dtype) for shape, dtype in scratch]
        + [pltpu.SemaphoreType.DMA((copies,))] * 2,
        compiler_params=pltpu.CompilerParams(
            collective_id=index, has_side_effects=True, vmem_limit_bytes=60 * 1024 * 1024
        ),
        name=kernel.__name__,
    )(*args)


def shards(hidden, w_in, embedding, depth_gain, w_out, codebook_ids):
    hid_count = lax.axis_size("hid")
    seq_count = lax.axis_size("seq")
    hid = lax.axis_index("hid")
    step = lax.rem(hid, 2)
    quarter = lax.div(hid, 2)
    width_in = hidden.shape[1] * hid_count
    depth = w_in.shape[2]
    entries = w_out.shape[2]
    frames = hidden.shape[0]
    own = codebook_ids.shape[1]
    owned = 2 * own

    ids = jnp.pad(codebook_ids, ((0, 6), (0, 128 - own)))
    proj, sq_all, w_full, ids_all = call(
        forward_kernel,
        0,
        [
            ((owned, depth), F32),
            ((8, 8, frames), F32),
            ((2, 4, 2, 2, 2, 16, entries), BF),
            ((2, 8, 128), jnp.int32),
        ],
        [
            ((4, 2, owned, depth), BF),
            ((7, owned, depth), BF),
            ((8, entries), BF),
            ((8, frames), F32),
        ],
        30,
        hidden,
        w_in,
        jnp.transpose(w_out, (1, 0, 2)),
        ids,
    )
    ids_own = jnp.concatenate([ids_all[0, :2, :own], ids_all[1, :2, :own]], axis=1)
    ratio_all = lax.rsqrt(jnp.sum(sq_all[:, 0, :], axis=0) / width_in + 1e-06)
    ratio = lax.dynamic_slice(ratio_all, (quarter * owned,), (owned,))
    looked = jnp.take(embedding[0], ids_own[0], axis=0).astype(F32)
    x_rows = ratio[:, None] * proj + jnp.where(step == 1, looked, 0.0)
    gain = lax.dynamic_slice(depth_gain, (step, 0), (1, depth))
    scale = lax.rsqrt(jnp.mean(x_rows * x_rows, axis=1, keepdims=True) + 1e-06)
    normed = (x_rows * scale * gain).astype(BF)
    head = w_full.reshape(depth, entries)
    logits = jnp.einsum("fd,dc->fc", normed, head, preferred_element_type=F32)
    targets = jnp.where(step == 1, ids_own[1], ids_own[0])
    lse = jax.nn.logsumexp(logits, axis=1)
    onehot = (targets[:, None] == jnp.arange(entries, dtype=jnp.int32)[None, :]).astype(F32)
    loss_weight = 2.0 * entries / (frames * seq_count)
    d_logit = ((jnp.exp(logits - lse[:, None]) - onehot) * loss_weight).astype(BF)
    out_part = jnp.einsum("fd,fc->dc", normed, d_logit, preferred_element_type=F32).astype(BF)
    d_norm = jnp.einsum("fc,dc->fd", d_logit, head, preferred_element_type=F32)
    gated = gain * d_norm
    d_x = scale * gated - x_rows * scale**3 * jnp.mean(gated * x_rows, axis=1, keepdims=True)
    d_ratio = jnp.sum(d_x * proj, axis=1)
    small = jnp.broadcast_to(d_ratio[None, :], (8, owned))

    d_all, small_all, out_sum = call(
        return_kernel,
        1,
        [
            ((2, 2, 2, owned, depth), BF),
            ((8, 8, owned), F32),
            ((2, 2, 2, 16, entries), BF),
        ],
        [
            ((2, 4, 2, 2, 16, entries), BF),
            ((3, 2, 2, 2, 16, entries), BF),
            ((3, 2, 2, 2, 16, entries), BF),
        ],
        24,
        d_x.astype(BF),
        small,
        out_part.reshape(2, 4, 2, 2, 2, 16, entries),
    )
    d_all = d_all.reshape(2, frames, depth)
    d_ratio_all = small_all[:, 0, :].reshape(4, 2, owned).sum(axis=1).reshape(frames)
    correction = ratio_all**3 * d_ratio_all / width_in
    scaled = (ratio_all[None, :, None] * d_all.astype(F32)).astype(BF)
    in_part = jnp.einsum("kfe,fd->ked", scaled, hidden, preferred_element_type=F32).astype(BF)
    back = jnp.einsum("kfe,kde->fd", d_all, w_in, preferred_element_type=F32)
    grad_hidden = (
        ratio_all[:, None] * back - correction[:, None] * hidden.astype(F32)
    ).astype(BF)

    units = hidden.shape[1]
    grad_in, grad_out = call(
        last_kernel,
        2,
        [((2, 64, units), F32), ((2, 8, entries), F32)],
        [
            ((2, 2, 4, 64, units), BF),
            ((3, 2, 2, 64, units), BF),
            ((3, 2, 2, 64, units), BF),
            ((2, 64, units), BF),
            ((2, 64, units), BF),
            ((3, 2, 16, entries), BF),
            ((16, entries), BF),
            ((16, entries), BF),
            ((16, entries), F32),
        ],
        16,
        in_part.reshape(2, 2, 4, 2, 64, units),
        out_sum,
    )
    return (
        grad_hidden,
        jnp.transpose(grad_in, (0, 2, 1)),
        jnp.transpose(grad_out, (1, 0, 2)),
    )


def solution(mesh):
    placed = (
        P("seq", "hid"),
        P(None, "hid", None),
        P(),
        P(),
        P(("seq", "hid"), None, None),
        P(None, ("seq", "hid")),
    )
    return jax.shard_map(
        shards,
        mesh=mesh,
        in_specs=placed,
        out_specs=(P("seq", "hid"), P(None, "hid", "seq"), P(("seq", "hid"), None, None)),
        check_vma=False,
    )
```

time: 625 us -> 167 us (0.27)
  waiting for transfers between devices: 477 us -> 0 us
  Pallas kernels: 0 us -> 131 us
  blocking collectives: 52.6 us -> 0 us
  local copies, waits for them, and re-layouts: 44.2 us -> 15.6 us
  matrix products: 30.7 us -> 14.8 us
  between operations: 16.6 us -> 0.77 us
    unnamed x7 -> x0, waiting for transfers between devices: 244 us -> none
    all_gather x2 -> x0, waiting for transfers between devices: 233 us -> none  [the longest x1 233 us: shards(): full_head = lax.all_gather(w_out, ('seq', 'hid'), axis=0, tiled=True)]
    pallas_call x0 -> x3, Pallas kernels: none -> 131 us  [call(): pl.pallas_call(kernel, out_shape=[jax.ShapeDtypeStruct(shape, dtype) for...]
    unnamed x2 -> x0, blocking collectives: 52.6 us -> none
    transpose x1 -> x0, local copies, waits for them, and re-layouts: 25.4 us -> none  [shards(): jnp.einsum('fkd,fkc->dkc', normed, d_logit, preferred_element_type=jnp.fl...]
    dot_general x6 -> x5, matrix products: 30.7 us -> 14.8 us  [the longest x1 3.68 us: shards(): back = jnp.einsum('kfe,kde->fd', d_all, w_in, preferred_element_type=F32)]
    unnamed x25 -> x13, local copies, waits for them, and re-layouts: 13.7 us -> 5.52 us
  transfers between devices with their start and end apart: 5 -> 0, of which waited for: 3 -> 0; matrix products, arithmetic and copies ran while one was open for 9% -> 0% of each run, Pallas kernels for 0% -> 0%
where the time goes in v1:
time: 167 us; the launch traced here: 166 us
  Pallas kernels  131 us (78%)
  local copies, waits for them, and re-layouts  15.6 us (9%)
  matrix products  14.8 us (9%)
  other arithmetic  3.86 us (2%)
    pallas_call x3, Pallas kernels, call(): pl.pallas_call(kernel, out_shape=[jax.ShapeDtypeStruct(shape, dtype) for...  131 us
    unnamed x13, local copies, waits for them, and re-layouts  5.52 us
    gather x1, local copies, waits for them, and re-layouts, shards(): looked = jnp.take(embedding[0], ids_own[0], axis=0).astype(F32)  3.77 us
    dot_general x1, matrix products, shards(): back = jnp.einsum('kfe,kde->fd', d_all, w_in, preferred_element_type=F32)  3.68 us
    dot_general x1, matrix products, shards(): jnp.einsum('fd,fc->dc', normed, d_logit, preferred_element_type=F32)  3.45 us
    dot_general x1, matrix products, shards(): logits = jnp.einsum('fd,dc->fc', normed, head, preferred_element_type=F32)  3.37 us

profile of v1, /device:TPU:0, one launch (start us, length us, event | category | flops | bytes accessed | tf_op | source)
XLA Modules:
  0.0 165.7 jit_solution(9599316012160449783)
XLA Ops:
  0.6 0.0 copy-start
  0.7 0.7 copy-done
  1.3 1.3 pad.4.ids
  2.6 1.5 copy.13
  4.1 67.3 %forward_kernel.1 = (f32[128,1024]{1,0:T(8,128)}, f32[8,8,512]{2,1,0:T(8,128)}, bf16[2,4,2,2,2,16,2048]{6,5,4,3,2,1,0:T(8,128)(2,1)}, s32[2,8,128]{2,1,0:T(8,128)}) custom-call(bf16[512,512]{1,0:T(8,128)(2,1)} %hidden.1, bf16[2,512,1024]{2,1,0:T(8,128)(2,1)} %w_in.1, bf16[2,8,2048]{2,1,0:T(8,128)(2,1)} %bitcast.50, s32[8,128]{1,0:T(8,128)} %pad.4.ids), custom_call_target="tpu_custom_call" | custom-call | tf_op jit(solution)/shard_map/forward_kernel/pallas_call | solution.py:299
  71.5 0.9 slice_reduce_fusion
  72.4 0.1 dynamic_slice.6
  72.5 0.7 slice_bitcast_fusion.1
  73.2 0.1 pad_add_fusion
  73.3 3.8 %gather_fusion = bf16[128,1024]{1,0:T(8,128)(2,1)S(1)} fusion(bf16[2048,1024]{1,0:T(8,128)(2,1)} %bitcast.48, s32[1024]{0:T(1024)S(1)} %pad_clamp_fusion), kind=kCustom, calls=%fused_computation | custom fusion | bytes 524800 | tf_op jit(solution)/shard_map/jit(_take)/gather | solution.py:351
  77.1 0.0 copy-start.1
  77.1 0.0 copy-start.2
  77.1 1.5 multiply_reduce_fusion.2
  78.6 3.4 %fusion.12 = (f32[128]{0:T(128)S(1)}, f32[128,2048]{1,0:T(8,128)S(1)}) fusion(bf16[1024,2048]{1,0:T(8,128)(2,1)} %bitcast.43, f32[1024]{0:T(1024)S(1)} %bitcast.51, f32[128]{0:T(128)S(1)} %get-tuple-element.29, bf16[128,1024]{1,0:T(8,128)(2,1)S(1)} %gather_fusion, pred[128]{0:T(512)(128)(4,1)S(1)} %compare_and_fusion, pred[]{:T(512)S(6)} %eq.8, ...), kind=kOutput, calls=%fused_computation.44 | convolution fusion | flops 538181504 | bytes 6035073 | tf_op jit(solution)/shard_map/fd,dc->fc/dot_general | solution.py:357
  82.0 0.3 exponential_reduce_fusion
  82.3 0.0 copy-done.1
  82.3 0.0 copy-done.2
  82.3 1.7 %multiply_reduce_fusion.1 = (f32[128]{0:T(128)S(1)}, f32[128,1024]{1,0:T(8,128)S(1)}) fusion(bf16[128,1024]{1,0:T(8,128)(2,1)S(1)} %gather_fusion, pred[128]{0:T(512)(128)(4,1)S(1)} %compare_and_fusion, pred[]{:T(512)S(6)} %eq.8, f32[128,1024]{1,0:T(8,128)S(1)} %copy-done.1, f32[128]{0:T(128)S(1)} %dynamic_slice.6, bf16[1024,2048]{1,0:T(8,128)(2,1)S(1)} %bitcast.44, ...), kind=kOutput, calls=%fused_computation.17 | convolution fusion | flops 539492224 | bytes 6559873 | tf_op jit(solution)/shard_map/fc,dc->fd/dot_general | solution.py:364
  84.0 1.0 multiply_reduce_fusion
  85.0 0.6 broadcast_in_dim.22.small
  85.6 3.5 %convolution_convert_fusion = bf16[1024,2048]{1,0:T(8,128)(2,1)} fusion(f32[1024]{0:T(1024)S(1)} %bitcast.53, f32[128]{0:T(128)S(1)} %get-tuple-element.29, f32[128,2048]{1,0:T(8,128)S(1)} %get-tuple-element.31, s32[128]{0:T(128)S(1)} %broadcast_select_fusion, f32[128]{0:T(128)S(1)} %log_add_fusion, f32[128,1024]{1,0:T(8,128)S(1)} %copy-done.1, ...), kind=kOutput, calls=%fused_computation.2 | convolution fusion | flops 541589504 | bytes 6035585 | tf_op jit(solution)/shard_map/fd,fc->dc/dot_general | solution.py:363
  89.0 0.0 copy-start.3
  89.0 38.9 %return_kernel.1 = (bf16[2,2,2,128,1024]{4,3,2,1,0:T(8,128)(2,1)}, f32[8,8,128]{2,1,0:T(8,128)}, bf16[2,2,2,16,2048]{4,3,2,1,0:T(8,128)(2,1)}) custom-call(bf16[128,1024]{1,0:T(8,128)(2,1)} %get-tuple-element.25.d_rows, f32[8,128]{1,0:T(8,128)} %broadcast_in_dim.22.small, bf16[2,4,2,2,2,16,2048]{6,5,4,3,2,1,0:T(8,128)(2,1)} %bitcast.42), custom_call_target="tpu_custom_call" | custom-call | tf_op jit(solution)/shard_map/return_kernel/pallas_call | solution.py:299
  127.9 0.8 slice.24
  128.7 0.0 copy-done.3
  128.7 0.0 copy-done.4
  128.7 3.7 %fusion.5 = bf16[512,512]{1,0:T(8,128)(2,1)} fusion(bf16[2,512,1024]{2,1,0:T(8,128)(2,1)} %bitcast.46, bf16[2,512,1024]{2,1,0:T(8,128)(2,1)S(1)} %copy-done.3, bf16[512,512]{1,0:T(8,128)(2,1)S(1)} %copy-done.4, f32[512]{0:T(512)S(1)} %fusion.8, f32[512]{0:T(512)S(1)} %add_rsqrt_fusion), kind=kOutput, calls=%fused_computation.9 | convolution fusion | flops 1075052544 | bytes 5246976 | tf_op jit(solution)/shard_map/kfe,kde->fd/dot_general | solution.py:393
  132.4 2.9 %copy.10 = bf16[2,512,1024]{1,2,0:T(8,128)(2,1)S(1)} copy(bf16[2,512,1024]{2,1,0:T(8,128)(2,1)} %bitcast.47) | data formatting | bytes 4194304 | tf_op jit(solution)/shard_map/reshape | solution.py:388
  135.2 2.6 %fusion.2 = bf16[2,1024,512]{2,1,0:T(8,128)(2,1)} fusion(bf16[2,512,1024]{1,2,0:T(8,128)(2,1)S(1)} %copy.10, f32[512]{0:T(512)S(1)} %add_rsqrt_fusion, bf16[512,512]{1,0:T(8,128)(2,1)S(1)} %copy-done.4), kind=kOutput, calls=%fused_computation.5 | convolution fusion | flops 1077936128 | bytes 4720640 | tf_op jit(solution)/shard_map/kfe,fd->ked/dot_general | solution.py:392
  137.9 24.5 %last_kernel.1 = (f32[2,64,512]{2,1,0:T(8,128)}, f32[2,8,2048]{2,1,0:T(8,128)}) custom-call(bf16[2,2,4,2,64,512]{5,4,3,2,1,0:T(8,128)(2,1)} %bitcast.45, bf16[2,2,2,16,2048]{4,3,2,1,0:T(8,128)(2,1)} %get-tuple-element.18.out_part), custom_call_target="tpu_custom_call" | custom-call | tf_op jit(solution)/shard_map/last_kernel/pallas_call | solution.py:299
  162.4 1.7 %copy.11 = f32[8,2,2048]{2,1,0:T(2,128)} copy(f32[8,2,2048]{2,0,1:T(8,128)} %bitcast.54) | data formatting | bytes 262144
  164.1 1.7 %copy.15 = f32[2,512,64]{1,2,0:T(8,128)} copy(f32[2,512,64]{1,2,0:T(8,128)} %bitcast.49) | data formatting | bytes 524288
  (13 shorter events, 0.1 us)
Async XLA Ops:
  0.6 0.7 copy-start
  77.1 5.2 %copy-start.1 = (f32[128,1024]{1,0:T(8,128)S(1)}, f32[128,1024]{1,0:T(8,128)}, u32[]{:S(2)}) copy-start(f32[128,1024]{1,0:T(8,128)} %get-tuple-element.13) | copy-start | bytes 1572868
  77.1 5.2 %copy-start.2 = (bf16[2,4,2,2,2,16,2048]{6,5,4,3,2,1,0:T(8,128)(2,1)S(1)}, bf16[2,4,2,2,2,16,2048]{6,5,4,3,2,1,0:T(8,128)(2,1)}, u32[]{:S(2)}) copy-start(bf16[2,4,2,2,2,16,2048]{6,5,4,3,2,1,0:T(8,128)(2,1)} %get-tuple-element.15) | copy-start | bytes 12582916
  89.0 39.7 %copy-start.3 = (bf16[2,512,1024]{2,1,0:T(8,128)(2,1)S(1)}, bf16[2,512,1024]{2,1,0:T(8,128)(2,1)}, u32[]{:S(2)}) copy-start(bf16[2,512,1024]{2,1,0:T(8,128)(2,1)} %w_in.1) | copy-start | bytes 6291460
  89.0 39.7 %copy-start.4 = (bf16[512,512]{1,0:T(8,128)(2,1)S(1)}, bf16[512,512]{1,0:T(8,128)(2,1)}, u32[]{:S(2)}) copy-start(bf16[512,512]{1,0:T(8,128)(2,1)} %hidden.1) | copy-start | bytes 1572868

commit v2 on v0

v2 whole, which is shorter than its diff:
```python
import functools

import jax
import jax.numpy as jnp
from jax import lax
from jax.experimental import pallas as pl
from jax.experimental.pallas import tpu as pltpu
from jax.sharding import PartitionSpec as P

MESH = pl.DeviceIdType.MESH
BF = jnp.bfloat16
F32 = jnp.float32
NT = (((1,), (1,)), ((), ()))


def place():
    s, h = lax.axis_index("seq"), lax.axis_index("hid")
    x_lo, y, c = lax.div(s, 8), lax.rem(lax.div(s, 2), 4), lax.rem(s, 2)
    return 2 * lax.div(h, 4) + x_lo, y, lax.rem(h, 4), c


def device(x, y, z, c):
    x, y, z, c = lax.rem(x, 4), lax.rem(y, 4), lax.rem(z, 4), lax.rem(c, 2)
    return (lax.rem(x, 2) * 8 + y * 2 + c, lax.div(x, 2) * 4 + z)


def greet(peers):
    barrier = pltpu.get_barrier_semaphore()
    for peer in peers:
        pl.semaphore_signal(barrier, inc=1, device_id=peer, device_id_type=MESH)
    pl.semaphore_wait(barrier, len(peers))


class Post:
    def __init__(self, send_sem, recv_sem):
        self.send_sem, self.recv_sem, self.copies = send_sem, recv_sem, []

    def send(self, src, dst, peer):
        i = len(self.copies)
        copy = pltpu.make_async_remote_copy(
            src_ref=src,
            dst_ref=dst,
            send_sem=self.send_sem.at[i],
            recv_sem=self.recv_sem.at[i],
            device_id=peer,
            device_id_type=MESH,
        )
        copy.start()
        self.copies.append(copy)
        return copy

    def close(self):
        for copy in self.copies:
            copy.wait_send()


def column(row):
    return jnp.transpose(jnp.broadcast_to(row, (128, 128)))


def at128(i):
    return pl.ds(pl.multiple_of(i * 128, 128), 128)


def kernel(loss_weight, width_in, hidden_in, w_in_in, embedding_in, gain_in, w_rows, ids, *rest):
    grad_hidden, grad_in, grad_out = rest[:3]
    (
        hidden, w_in, embedding, part, z_got, x_send, x_got, w_pair, w_full, ids_all,
        sq_mine, sq_all, ratio_rows, ratio_col, scaled, looked, x_rows, proj, normed, turned, logits,
        d_logit, scale_col, d_norm, dr_col, d_turn, d_all, small, small_all, corr_col,
        gp, gp_c, gp_y, gp_yg, gp_sum, gp_xg, gp_z, gp_zg, gp_rows, gp_pair,
        ip, ip_c, ip_y, ip_yg, ip_x, ip_xg, local_sem, send_sem, recv_sem,
    ) = rest[3:]
    x, y, z, c = place()
    x_lo, x_hi, step, zh = lax.rem(x, 2), lax.div(x, 2), lax.rem(z, 2), lax.div(z, 2)
    hid = x_hi * 4 + z
    quarter = x_hi * 2 + zh
    pair = device(x, y, z + 1 - 2 * step, c)
    across = device(x, y, z + 2, c)
    far = device(x + 2, y, z, c)
    twin = device(x, y, z, c + 1)
    beside = device(x + 1 - 2 * x_lo, y, z, c)
    xs = {d: device(x + d, y, z, c) for d in (1, 2, 3)}
    ys = {d: device(x, y + d, z, c) for d in (1, 2, 3)}
    zs = {d: device(x, y, z + d, c) for d in (1, 2, 3)}
    hid_peers = [device(x + dx, y, z + dz, c) for dz in (2, 1, 3, 0) for dx in (2, 0) if dx + dz]

    loads = [
        pltpu.make_async_copy(src, dst, local_sem.at[i])
        for i, (src, dst) in enumerate(
            ((hidden_in, hidden), (w_in_in, w_in), (embedding_in, embedding))
        )
    ]
    for load in loads:
        load.start()
    greet(hid_peers + [xs[1], xs[3]] + list(ys.values()) + [twin])
    post = Post(send_sem, recv_sem)

    w_swap = post.send(w_rows.at[1 - step], w_pair, pair)
    ids_swap = post.send(ids, ids_all.at[step], pair)
    ids_all[step] = ids[...]
    loads[0].wait()
    h = hidden[...].astype(F32)
    h2 = h * h
    top = h2.astype(BF)
    low = (h2 - top.astype(F32)).astype(BF)
    ones = jnp.ones((8, h2.shape[1]), BF)
    sq_mine[...] = lax.dot_general(ones, top, NT, preferred_element_type=F32) + lax.dot_general(
        ones, low, NT, preferred_element_type=F32
    )
    sq_all[hid] = sq_mine[...]
    loads[1].wait()

    def chunk(dz):
        to_z = lax.rem(z + dz, 4)
        rows = [hidden[at128(fx * 2 + lax.div(to_z, 2)), :] for fx in range(2)]
        product = jnp.dot(
            jnp.concatenate(rows, axis=0), w_in[lax.rem(to_z, 2)], preferred_element_type=F32
        ).astype(BF)
        part[dz, 0] = product[:128]
        part[dz, 1] = product[128:]

    chunk(2)
    sq_copies = [post.send(sq_mine, sq_all.at[hid], peer) for peer in hid_peers]
    z_copies = [post.send(part.at[2], z_got.at[0], zs[2])]
    w_swap.wait_recv()
    mine = w_rows[step].astype(F32)
    other = w_pair[...].astype(F32)
    first = jnp.where(step == 0, mine, other)
    second = jnp.where(step == 0, other, mine)
    w_full[x_lo, y, c, x_hi, zh] = jnp.concatenate([first, second], axis=0).astype(BF)
    chunk(1)
    block = w_full.at[x_lo, y, c, x_hi, zh]
    w_across = post.send(block, block, across)
    wa_x = [post.send(block, block, xs[d]) for d in (1, 3, 2)]
    z_copies.append(post.send(part.at[1], z_got.at[1], zs[1]))
    chunk(3)
    z_copies.append(post.send(part.at[3], z_got.at[2], zs[3]))
    w_across.wait_recv()
    block = w_full.at[x_lo, y, c, x_hi, 1 - zh]
    wb_y = [post.send(block, block, ys[d]) for d in (1, 3, 2)]
    chunk(0)
    for copy in wa_x:
        copy.wait_recv()
    line = w_full.at[:, y, c, :, zh]
    wa_y = {d: post.send(line, line, ys[d]) for d in (2, 1, 3)}
    w_twin = [post.send(line, line, twin)]
    for copy in wb_y:
        copy.wait_recv()
    line = w_full.at[x_lo, :, c, x_hi, 1 - zh]
    wb_x = {d: post.send(line, line, xs[d]) for d in (2, 1, 3)}
    w_twin.append(post.send(line, line, twin))

    for copy in sq_copies:
        copy.wait_recv()
    squares = sq_all[0]
    for i in range(1, 8):
        squares = squares + sq_all[i]
    ratio_rows[...] = lax.rsqrt(squares / width_in + 1e-06)
    for q in range(4):
        wide = column(ratio_rows[0:1, q * 128 : (q + 1) * 128])
        scaled[q * 128 : (q + 1) * 128, :] = (
            hidden[q * 128 : (q + 1) * 128, :].astype(F32) * wide[:, :1]
        ).astype(BF)
    ratio_col[...] = column(ratio_rows[0:1, at128(quarter)])
    ids_swap.wait_recv()

    def tokens(k):
        halves = [column(ids_all[i, k : k + 1, :].astype(F32))[:64, :1] for i in range(2)]
        return jnp.concatenate(halves, axis=0).astype(jnp.int32)

    previous, current = tokens(0), tokens(1)
    target = jnp.where(step == 1, current, previous)
    entries = logits.shape[1]
    lanes = lax.broadcasted_iota(jnp.int32, (128, entries), 1)
    loads[2].wait()
    pick = jnp.where(lanes == previous, 1.0, 0.0).astype(BF)
    live = step.astype(F32)
    for n in range(2):
        cols = slice(n * 512, (n + 1) * 512)
        looked[:, cols] = jnp.dot(pick, embedding[:, cols], preferred_element_type=F32) * live

    for copy in z_copies:
        copy.wait_recv()

    def z_sum(fx, rows):
        value = part[0, fx, rows, :].astype(F32)
        for i in range(3):
            value = value + z_got[i, fx, rows, :].astype(F32)
        return value

    @pl.loop(0, 8)
    def to_far(i):
        rows = pl.ds(pl.multiple_of(i * 16, 16), 16)
        x_send[rows, :] = z_sum(1 - x_hi, rows).astype(BF)

    x_copy = post.send(x_send, x_got, far)
    for d in (1, 3, 2):
        wa_y[d].wait_recv()
        line = w_full.at[:, lax.rem(y + 4 - d, 4), c, :, zh]
        w_twin.append(post.send(line, line, twin))
    for d in (1, 3, 2):
        wb_x[d].wait_recv()
        from_x = lax.rem(x + 4 - d, 4)
        line = w_full.at[lax.rem(from_x, 2), :, c, lax.div(from_x, 2), 1 - zh]
        w_twin.append(post.send(line, line, twin))
    x_copy.wait_recv()
    gain = gain_in[pl.ds(step, 1), :]

    @pl.loop(0, 8)
    def norm(i):
        rows = pl.ds(pl.multiple_of(i * 16, 16), 16)
        p = z_sum(x_hi, rows) + x_got[rows, :].astype(F32)
        value = ratio_col[rows, :1] * p + looked[rows, :]
        scale = lax.rsqrt(jnp.mean(value * value, axis=1, keepdims=True) + 1e-06)
        proj[rows, :] = p
        x_rows[rows, :] = value
        scale_col[rows, :] = jnp.broadcast_to(scale, (16, 128))
        normed[rows, :] = (value * scale * gain).astype(BF)

    for copy in w_twin:
        copy.wait_recv()

    depth = normed.shape[1]
    for n in range(4):
        cols = slice(n * 512, (n + 1) * 512)
        head = w_full[:, :, :, :, :, :, cols].reshape(depth, 512)
        logits[:, cols] = jnp.dot(normed[...], head, preferred_element_type=F32)
    for k in range(8):
        cols = slice(k * 128, (k + 1) * 128)
        turned[cols, :] = jnp.transpose(normed[:, cols].astype(F32)).astype(BF)
    scale_t = jnp.broadcast_to(target.astype(F32), (128, 128))
    dr_col[...] = scale_t

    @pl.loop(0, 8)
    def soft(i):
        rows = pl.ds(pl.multiple_of(i * 16, 16), 16)
        value = logits[rows, :]
        value = jnp.exp(value - jnp.max(value, axis=1, keepdims=True))
        share = value * (1.0 / jnp.sum(value, axis=1, keepdims=True))
        hot = lax.broadcasted_iota(jnp.int32, (16, entries), 1) == dr_col[rows, :1].astype(
            jnp.int32
        )
        d_logit[rows, :] = ((share - jnp.where(hot, 1.0, 0.0)) * loss_weight).astype(BF)

    for k in range(4):
        a, b = k // 2, (k % 2) * 2
        head = w_full[a, b : b + 2].reshape(256, entries)
        d_norm[:, k * 256 : (k + 1) * 256] = lax.dot_general(
            d_logit[...], head, NT, preferred_element_type=F32
        )

    @pl.loop(0, 8)
    def unnorm(i):
        rows = pl.ds(pl.multiple_of(i * 16, 16), 16)
        value, scale = x_rows[rows, :], scale_col[rows, :1]
        gated = gain * d_norm[rows, :]
        inner = jnp.mean(gated * value, axis=1, keepdims=True)
        d_x = scale * gated - value * (scale * scale * scale * inner)
        d_norm[rows, :] = d_x
        total = jnp.sum(d_x * proj[rows, :], axis=1, keepdims=True)
        dr_col[rows, :] = jnp.broadcast_to(total, (16, 128))

    small[...] = jnp.transpose(dr_col[...])[:8]
    for k in range(8):
        cols = slice(k * 128, (k + 1) * 128)
        d_turn[cols, :] = jnp.transpose(d_norm[:, cols]).astype(BF)
    slab = d_all.at[step, :, at128(quarter)]
    rows_copies = []
    for peer in hid_peers:
        rows_copies.append(post.send(d_turn, slab, peer))
        rows_copies.append(post.send(small, small_all.at[hid], peer))
    d_all[step, :, at128(quarter)] = d_turn[...]
    small_all[hid] = small[...]

    order = (2, 1, 3, 0)
    gp_swap = []
    for d in order:
        to_y = lax.rem(y + d, 4)
        for a in range(2):
            rows = at128(a * 4 + to_y)
            gp[a, to_y] = (
                jnp.dot(turned[rows, :], d_logit[...], preferred_element_type=F32)
                .astype(BF)
                .reshape(2, 2, 2, 16, entries)
            )
        gp_swap.append(post.send(gp.at[:, to_y, 1 - c], gp_c.at[:, to_y], twin))
    gp_ys = []
    for i, d in enumerate(order[:3]):
        gp_swap[i].wait_recv()
        to_y = lax.rem(y + d, 4)

        @pl.loop(0, 8)
        def add(j):
            a, b, e = lax.div(j, 4), lax.rem(lax.div(j, 2), 2), lax.rem(j, 2)
            gp_y[i, a, b, e] = (
                gp[a, to_y, c, b, e].astype(F32) + gp_c[a, to_y, b, e].astype(F32)
            ).astype(BF)

        gp_ys.append(post.send(gp_y.at[i], gp_yg.at[i], ys[d]))
    gp_swap[3].wait_recv()

    for copy in rows_copies:
        copy.wait_recv()
    ip_swap = []
    for d in order:
        to_y = lax.rem(y + d, 4)
        rows = [d_all[s, at128(a * 4 + to_y), :] for s in range(2) for a in range(2)]
        product = jnp.dot(
            jnp.concatenate(rows, axis=0), scaled[...], preferred_element_type=F32
        ).astype(BF)
        for s in range(2):
            for a in range(2):
                for e in range(2):
                    start = (s * 2 + a) * 128 + e * 64
                    ip[s, a, to_y, e] = product[start : start + 64]
        ip_swap.append(post.send(ip.at[:, :, to_y, 1 - c], ip_c.at[:, :, to_y], twin))
    ip_ys = []
    for i, d in enumerate(order[:3]):
        ip_swap[i].wait_recv()
        to_y = lax.rem(y + d, 4)

        @pl.loop(0, 4)
        def add_in(j):
            a, b = lax.div(j, 2), lax.rem(j, 2)
            ip_y[i, a, b] = (
                ip[a, b, to_y, c].astype(F32) + ip_c[a, b, to_y].astype(F32)
            ).astype(BF)

        ip_ys.append(post.send(ip_y.at[i], ip_yg.at[i], ys[d]))
    ip_swap[3].wait_recv()

    for copy in gp_ys:
        copy.wait_recv()

    @pl.loop(0, 8)
    def total(j):
        a, b, e = lax.div(j, 4), lax.rem(lax.div(j, 2), 2), lax.rem(j, 2)
        value = gp[a, y, c, b, e].astype(F32) + gp_c[a, y, b, e].astype(F32)
        for i in range(3):
            value = value + gp_yg[i, a, b, e].astype(F32)
        gp_sum[a, b, e] = value.astype(BF)

    gp_xs = []
    for i, d in enumerate(order[:3]):
        to_x = lax.rem(x + d, 4)
        gp_xs.append(
            post.send(gp_sum.at[lax.rem(to_x, 2), lax.div(to_x, 2)], gp_xg.at[i], xs[d])
        )

    ratio_row = ratio_rows[0:1, :]
    for q in range(4):
        cols = slice(q * 128, (q + 1) * 128)
        r = ratio_rows[0:1, cols]
        total_dr = small_all[2 * q, 0:1, :] + small_all[2 * q + 1, 0:1, :]
        corr_col[cols, :] = column(r * r * r * total_dr * (1.0 / width_in))

    def back(k):
        cols = slice(k * 128, (k + 1) * 128)
        value = jnp.dot(w_in[0, cols, :], d_all[0], preferred_element_type=F32) + jnp.dot(
            w_in[1, cols, :], d_all[1], preferred_element_type=F32
        )
        grad_hidden[:, cols] = (
            jnp.transpose(value * ratio_row)
            - corr_col[:, :1] * hidden[:, cols].astype(F32)
        ).astype(BF)

    back(0)
    back(1)
    for copy in gp_xs:
        copy.wait_recv()

    def out_block(e):
        value = gp_sum[x_lo, x_hi, e].astype(F32)
        for i in range(3):
            value = value + gp_xg[i, e].astype(F32)
        return value

    gp_z[...] = out_block(1 - zh).astype(BF)
    gp_across = post.send(gp_z, gp_zg, across)
    back(2)
    for copy in ip_ys:
        copy.wait_recv()

    def in_block(a, b):
        value = ip[a, b, y, c].astype(F32) + ip_c[a, b, y].astype(F32)
        for i in range(3):
            value = value + ip_yg[i, a, b].astype(F32)
        return value

    for a in range(2):
        ip_x[a] = in_block(a, 1 - x_lo).astype(BF)
    ip_beside = post.send(ip_x, ip_xg, beside)
    gp_across.wait_recv()
    gp_rows[...] = out_block(zh) + gp_zg[...].astype(F32)
    theirs = gp_rows.at[pl.ds(pl.multiple_of((1 - step) * 8, 8), 8), :]
    gp_swap_rows = post.send(theirs, gp_pair, pair)
    back(3)
    own = [in_block(a, x_lo) for a in range(2)]
    ip_beside.wait_recv()
    both = jnp.concatenate([own[a] + ip_xg[a].astype(F32) for a in range(2)], axis=0)
    both = jnp.transpose(both)
    grad_in[0] = both[:, :64]
    grad_in[1] = both[:, 64:]
    gp_swap_rows.wait_recv()
    grad_out[step] = gp_rows[pl.ds(pl.multiple_of(step * 8, 8), 8), :]
    grad_out[1 - step] = gp_pair[...]
    post.close()


def shards(hidden, w_in, embedding, depth_gain, w_out, codebook_ids):
    hid_count = lax.axis_size("hid")
    seq_count = lax.axis_size("seq")
    width_in = hidden.shape[1] * hid_count
    depth = w_in.shape[2]
    entries = w_out.shape[2]
    frames, units = hidden.shape
    own = codebook_ids.shape[1]
    loss_weight = 2.0 * entries / (frames * seq_count)
    ids = jnp.pad(codebook_ids, ((0, 6), (0, 128 - own)))
    vmem = pl.BlockSpec(memory_space=pltpu.VMEM)
    anywhere = pl.BlockSpec(memory_space=pl.ANY)
    scratch = [
        ((frames, units), BF),
        ((2, units, depth), BF),
        ((entries, depth), BF),
        ((4, 2, 128, depth), BF),
        ((3, 2, 128, depth), BF),
        ((128, depth), BF),
        ((128, depth), BF),
        ((8, entries), BF),
        ((2, 4, 2, 2, 2, 16, entries), BF),
        ((2, 8, 128), jnp.int32),
        ((8, frames), F32),
        ((8, 8, frames), F32),
        ((8, frames), F32),
        ((128, 128), F32),
        ((frames, units), BF),
        ((128, depth), F32),
        ((128, depth), F32),
        ((128, depth), F32),
        ((128, depth), BF),
        ((depth, 128), BF),
        ((128, entries), F32),
        ((128, entries), BF),
        ((128, 128), F32),
        ((128, depth), F32),
        ((128, 128), F32),
        ((depth, 128), BF),
        ((2, depth, frames), BF),
        ((8, 128), F32),
        ((8, 8, 128), F32),
        ((frames, 128), F32),
        ((2, 4, 2, 2, 2, 16, entries), BF),
        ((2, 4, 2, 2, 16, entries), BF),
        ((3, 2, 2, 2, 16, entries), BF),
        ((3, 2, 2, 2, 16, entries), BF),
        ((2, 2, 2, 16, entries), BF),
        ((3, 2, 16, entries), BF),
        ((16, entries), BF),
        ((16, entries), BF),
        ((16, entries), F32),
        ((8, entries), F32),
        ((2, 2, 4, 2, 64, units), BF),
        ((2, 2, 4, 64, units), BF),
        ((3, 2, 2, 64, units), BF),
        ((3, 2, 2, 64, units), BF),
        ((2, 64, units), BF),
        ((2, 64, units), BF),
    ]
    grad_hidden, grad_in, grad_out = pl.pallas_call(
        functools.partial(kernel, loss_weight, width_in),
        out_shape=[
            jax.ShapeDtypeStruct((frames, units), BF),
            jax.ShapeDtypeStruct((2, units, 64), F32),
            jax.ShapeDtypeStruct((2, 8, entries), F32),
        ],
        in_specs=[anywhere] * 3 + [vmem] * 3,
        out_specs=[vmem] * 3,
        scratch_shapes=[pltpu.VMEM(shape, dtype) for shape, dtype in scratch]
        + [
            pltpu.SemaphoreType.DMA((3,)),
            pltpu.SemaphoreType.DMA((80,)),
            pltpu.SemaphoreType.DMA((80,)),
        ],
        compiler_params=pltpu.CompilerParams(
            collective_id=0, has_side_effects=True, vmem_limit_bytes=60 * 1024 * 1024
        ),
        name="whole",
    )(hidden, w_in, embedding[0], depth_gain, jnp.transpose(w_out, (1, 0, 2)), ids)
    return grad_hidden, grad_in, jnp.transpose(grad_out, (1, 0, 2))


def solution(mesh):
    placed = (
        P("seq", "hid"),
        P(None, "hid", None),
        P(),
        P(),
        P(("seq", "hid"), None, None),
        P(None, ("seq", "hid")),
    )
    return jax.shard_map(
        shards,
        mesh=mesh,
        in_specs=placed,
        out_specs=(P("seq", "hid"), P(None, "hid", "seq"), P(("seq", "hid"), None, None)),
        check_vma=False,
    )
```

time: 625 us -> 113 us (0.18)
  waiting for transfers between devices: 477 us -> 0 us
  Pallas kernels: 0 us -> 104 us
  blocking collectives: 52.6 us -> 0 us
  local copies, waits for them, and re-layouts: 44.2 us -> 8.22 us
  matrix products: 30.7 us -> 0 us
  between operations: 16.6 us -> 0.64 us
    unnamed x7 -> x0, waiting for transfers between devices: 244 us -> none
    all_gather x2 -> x0, waiting for transfers between devices: 233 us -> none  [the longest x1 233 us: shards(): full_head = lax.all_gather(w_out, ('seq', 'hid'), axis=0, tiled=True)]
    pallas_call x0 -> x1, Pallas kernels: none -> 104 us  [shards(): pl.pallas_call(functools.partial(kernel, loss_weight, width_in), out_shap...]
    unnamed x2 -> x0, blocking collectives: 52.6 us -> none
    dot_general x6 -> x0, matrix products: 30.7 us -> none  [the longest x1 9.41 us: shards(): jnp.einsum('fkd,fkc->dkc', normed, d_logit, preferred_element_type=jnp.fl...]
    transpose x1 -> x0, local copies, waits for them, and re-layouts: 25.4 us -> none  [shards(): jnp.einsum('fkd,fkc->dkc', normed, d_logit, preferred_element_type=jnp.fl...]
    unnamed x25 -> x4, local copies, waits for them, and re-layouts: 13.7 us -> 6.95 us
  transfers between devices with their start and end apart: 5 -> 0, of which waited for: 3 -> 0; matrix products, arithmetic and copies ran while one was open for 9% -> 0% of each run, Pallas kernels for 0% -> 0%
where the time goes in v2:
time: 113 us
  Pallas kernels  104 us (92%)
  local copies, waits for them, and re-layouts  8.22 us (7%)
    pallas_call x1, Pallas kernels, shards(): pl.pallas_call(functools.partial(kernel, loss_weight, width_in), out_shap...  104 us
    unnamed x4, local copies, waits for them, and re-layouts  6.95 us

profile of v2, /device:TPU:0, one launch (start us, length us, event | category | flops | bytes accessed | tf_op | source)
XLA Modules:
  0.0 112.6 jit_solution(6527708141048568789)
XLA Ops:
  0.6 1.3 %pad.4.ids = s32[8,128]{1,0:T(8,128)} pad(s32[2,64]{1,0:T(2,128)} %param.11, s32[]{:T(128)} %constant.0.clone.1), padding=0_6x0_64 | pad | bytes 4612 | tf_op jit(solution)/shard_map/jit(_pad)/pad | solution.py:420
  1.9 1.5 %copy.13 = bf16[8,2,2048]{2,0,1:T(8,128)(2,1)} copy(bf16[8,2,2048]{2,1,0:T(2,128)(2,1)} %param.10) | data formatting | bytes 131072 | tf_op args[4]
  3.4 103.7 %whole.1 = (bf16[512,512]{1,0:T(8,128)(2,1)}, f32[2,512,64]{2,1,0:T(8,128)}, f32[2,8,2048]{2,1,0:T(8,128)}) custom-call(bf16[512,512]{1,0:T(8,128)(2,1)} %hidden_in.1, bf16[2,512,1024]{2,1,0:T(8,128)(2,1)} %w_in_in.1, bf16[2048,1024]{1,0:T(8,128)(2,1)} %bitcast.5, f32[2,1024]{1,0:T(2,128)} %gain_in.1, bf16[2,8,2048]{2,1,0:T(8,128)(2,1)} %bitcast.6, ...), custom_call_target="tpu_custom_call" | custom-call | tf_op jit(solution)/shard_map/whole/pallas_call | solution.py:471
  107.1 1.7 %copy.11 = f32[8,2,2048]{2,1,0:T(2,128)} copy(f32[8,2,2048]{2,0,1:T(8,128)} %bitcast.7) | data formatting | bytes 262144
  108.8 1.9 %copy.10 = f32[2,512,64]{1,2,0:T(8,128)} copy(f32[2,512,64]{2,1,0:T(8,128)} %get-tuple-element.10) | data formatting | bytes 524288
  110.7 1.9 %copy.15 = bf16[512,512]{1,0:T(8,128)(2,1)} copy(bf16[512,512]{1,0:T(8,128)(2,1)} %get-tuple-element.15) | data formatting | bytes 1048576

commit v3 on v2

v3 whole, which is shorter than its diff:
```python
import functools

import jax
import jax.numpy as jnp
from jax import lax
from jax.experimental import pallas as pl
from jax.experimental.pallas import tpu as pltpu
from jax.sharding import PartitionSpec as P

MESH = pl.DeviceIdType.MESH
BF = jnp.bfloat16
F32 = jnp.float32
NT = (((1,), (1,)), ((), ()))


def place():
    s, h = lax.axis_index("seq"), lax.axis_index("hid")
    x_lo, y, c = lax.div(s, 8), lax.rem(lax.div(s, 2), 4), lax.rem(s, 2)
    return 2 * lax.div(h, 4) + x_lo, y, lax.rem(h, 4), c


def device(x, y, z, c):
    x, y, z, c = lax.rem(x, 4), lax.rem(y, 4), lax.rem(z, 4), lax.rem(c, 2)
    return (lax.rem(x, 2) * 8 + y * 2 + c, lax.div(x, 2) * 4 + z)


def greet(peers):
    barrier = pltpu.get_barrier_semaphore()
    for peer in peers:
        pl.semaphore_signal(barrier, inc=1, device_id=peer, device_id_type=MESH)
    pl.semaphore_wait(barrier, len(peers))


class Post:
    def __init__(self, send_sem, recv_sem):
        self.send_sem, self.recv_sem, self.copies = send_sem, recv_sem, []

    def send(self, src, dst, peer):
        i = len(self.copies)
        copy = pltpu.make_async_remote_copy(
            src_ref=src,
            dst_ref=dst,
            send_sem=self.send_sem.at[i],
            recv_sem=self.recv_sem.at[i],
            device_id=peer,
            device_id_type=MESH,
        )
        copy.start()
        self.copies.append(copy)
        return copy

    def close(self):
        for copy in self.copies:
            copy.wait_send()


def column(row):
    return jnp.transpose(jnp.broadcast_to(row, (128, 128)))


def at128(i):
    return pl.ds(pl.multiple_of(i * 128, 128), 128)


def kernel(loss_weight, width_in, hidden_in, w_in_in, embedding_in, gain_in, w_out, ids, *rest):
    grad_hidden, grad_in, grad_out = rest[:3]
    (
        hidden, w_in, embedding, part, relay, relay_sum, z_got, x_send, x_got,
        w_rows, w_got, w_full, ids_mine, ids_all,
        sq_mine, sq_all, ratio_rows, ratio_col, scaled, looked, x_rows, proj, normed, turned, logits,
        d_logit, scale_col, d_norm, dr_col, d_turn, d_all, small, small_all, corr_col,
        gp, gp_c, ga_y, ga_yg, ga_sum, ga_xg, gb_x, gb_xg, gb_sum, gb_yg, gp_z, gp_zg, gp_rows, gp_pair,
        ip, ip_c, ip_y, ip_yg, ip_x, ip_xg, local_sem, send_sem, recv_sem,
    ) = rest[3:]
    x, y, z, c = place()
    x_lo, x_hi, step, zh = lax.rem(x, 2), lax.div(x, 2), lax.rem(z, 2), lax.div(z, 2)
    hid = x_hi * 4 + z
    quarter, far_quarter = x_hi * 2 + zh, (1 - x_hi) * 2 + zh
    pair = device(x, y, z + 1 - 2 * step, c)
    far = device(x + 2, y, z, c)
    twin = device(x, y, z, c + 1)
    beside = device(x + 1 - 2 * x_lo, y, z, c)
    xs = {d: device(x + d, y, z, c) for d in (1, 2, 3)}
    ys = {d: device(x, y + d, z, c) for d in (1, 2, 3)}
    zs = {d: device(x, y, z + d, c) for d in (1, 2, 3)}
    hid_peers = [device(x + dx, y, z + dz, c) for dz in (2, 1, 3, 0) for dx in (2, 0) if dx + dz]
    order = (2, 1, 3, 0)

    loads = [
        pltpu.make_async_copy(src, dst, local_sem.at[i])
        for i, (src, dst) in enumerate(
            ((hidden_in, hidden), (w_in_in, w_in), (embedding_in, embedding))
        )
    ]
    for load in loads:
        load.start()
    w_rows[0] = w_out[:, 0, :]
    w_rows[1] = w_out[:, 1, :]
    ids_mine[...] = jnp.zeros_like(ids_mine)
    ids_mine[0:2, 0:64] = ids[...]
    greet(hid_peers + [xs[1], xs[3]] + list(ys.values()) + [twin])
    post = Post(send_sem, recv_sem)

    w_z = [post.send(w_rows.at[(step + d) % 2], w_got.at[z], zs[d]) for d in (2, 1, 3)]
    ids_swap = post.send(ids_mine, ids_all.at[step], pair)
    ids_all[step] = ids_mine[...]
    w_got[z] = w_rows[step]
    loads[0].wait()
    h = hidden[...].astype(F32)
    h2 = h * h
    top = h2.astype(BF)
    low = (h2 - top.astype(F32)).astype(BF)
    ones = jnp.ones((8, h2.shape[1]), BF)
    sq_mine[...] = lax.dot_general(ones, top, NT, preferred_element_type=F32) + lax.dot_general(
        ones, low, NT, preferred_element_type=F32
    )
    sq_all[hid] = sq_mine[...]
    loads[1].wait()

    def chunk(dz):
        to_z = lax.rem(z + dz, 4)
        rows = [hidden[at128(fx * 2 + lax.div(to_z, 2)), :] for fx in range(2)]
        product = jnp.dot(
            jnp.concatenate(rows, axis=0), w_in[lax.rem(to_z, 2)], preferred_element_type=F32
        ).astype(BF)
        part[dz, 0] = product[:128]
        part[dz, 1] = product[128:]

    halves = (pl.ds(0, 64), pl.ds(64, 64))
    relays, z_copies = [[], []], [[], []]

    def send_opposite(p):
        rows = halves[p]
        relays[p].append(post.send(part.at[2, 0, rows], relay.at[0, rows], zs[1]))
        relays[p].append(post.send(part.at[2, 1, rows], relay.at[1, rows], zs[3]))

    def send_direct(p, dz):
        rows, fx, slot = halves[p], (1 if dz == 1 else 0), (0 if dz == 1 else 1)
        z_copies[p].append(post.send(part.at[dz, fx, rows], z_got.at[slot, fx, rows], zs[dz]))

    def send_sums(p):
        for fx, dz in ((0, 1), (1, 3)):
            rows = halves[p]
            relays[p][fx].wait_recv()
            relay_sum[fx, rows, :] = (
                part[dz, fx, rows, :].astype(F32) + relay[fx, rows, :].astype(F32)
            ).astype(BF)
            z_copies[p].append(
                post.send(relay_sum.at[fx, rows], z_got.at[fx, fx, rows], zs[dz])
            )

    chunk(2)
    send_opposite(0)
    sq_copies = [post.send(sq_mine, sq_all.at[hid], peer) for peer in hid_peers]
    chunk(1)
    send_direct(0, 1)
    chunk(3)
    send_direct(0, 3)
    send_opposite(1)
    send_direct(1, 1)
    send_direct(1, 3)
    for copy in w_z:
        copy.wait_recv()
    for e in range(2):
        both = [w_got[2 * e + i].astype(F32) for i in range(2)]
        w_full[x_lo, y, c, x_hi, e] = jnp.concatenate(both, axis=0).astype(BF)
    block = w_full.at[x_lo, y, c, x_hi, zh]
    wa_x = [post.send(block, block, xs[d]) for d in (1, 3, 2)]
    block = w_full.at[x_lo, y, c, x_hi, 1 - zh]
    wb_y = [post.send(block, block, ys[d]) for d in (1, 3, 2)]
    chunk(0)
    send_sums(0)
    for copy in wa_x:
        copy.wait_recv()
    line = w_full.at[:, y, c, :, zh]
    wa_y = {d: post.send(line, line, ys[d]) for d in (2, 1, 3)}
    w_twin = [post.send(line, line, twin)]
    for copy in wb_y:
        copy.wait_recv()
    line = w_full.at[x_lo, :, c, x_hi, 1 - zh]
    wb_x = {d: post.send(line, line, xs[d]) for d in (2, 1, 3)}
    w_twin.append(post.send(line, line, twin))
    send_sums(1)

    for copy in sq_copies:
        copy.wait_recv()
    squares = sq_all[0]
    for i in range(1, 8):
        squares = squares + sq_all[i]
    ratio_rows[...] = lax.rsqrt(squares / width_in + 1e-06)
    for q in range(4):
        wide = column(ratio_rows[0:1, q * 128 : (q + 1) * 128])
        scaled[q * 128 : (q + 1) * 128, :] = (
            hidden[q * 128 : (q + 1) * 128, :].astype(F32) * wide[:, :1]
        ).astype(BF)
    ratio_col[...] = column(ratio_rows[0:1, at128(quarter)])
    ids_swap.wait_recv()

    def tokens(k):
        parts = [column(ids_all[i, k : k + 1, :].astype(F32))[:64, :1] for i in range(2)]
        return jnp.concatenate(parts, axis=0).astype(jnp.int32)

    previous, current = tokens(0), tokens(1)
    target = jnp.where(step == 1, current, previous)
    entries = logits.shape[1]
    lanes = lax.broadcasted_iota(jnp.int32, (128, entries), 1)
    loads[2].wait()
    pick = jnp.where(lanes == previous, 1.0, 0.0).astype(BF)
    live = step.astype(F32)
    for n in range(2):
        cols = slice(n * 512, (n + 1) * 512)
        looked[:, cols] = jnp.dot(pick, embedding[:, cols], preferred_element_type=F32) * live

    def z_sum(fx, rows):
        return (
            part[0, fx, rows, :].astype(F32)
            + z_got[0, fx, rows, :].astype(F32)
            + z_got[1, fx, rows, :].astype(F32)
        )

    x_copies = []
    for p in range(2):
        for copy in z_copies[p]:
            copy.wait_recv()

        @pl.loop(p * 4, p * 4 + 4, unroll=True)
        def to_far(i):
            rows = pl.ds(pl.multiple_of(i * 16, 16), 16)
            x_send[rows, :] = z_sum(1 - x_hi, rows).astype(BF)

        x_copies.append(post.send(x_send.at[halves[p]], x_got.at[halves[p]], far))
    for d in (1, 3, 2):
        wa_y[d].wait_recv()
        line = w_full.at[:, lax.rem(y + 4 - d, 4), c, :, zh]
        w_twin.append(post.send(line, line, twin))
    for d in (1, 3, 2):
        wb_x[d].wait_recv()
        from_x = lax.rem(x + 4 - d, 4)
        line = w_full.at[lax.rem(from_x, 2), :, c, lax.div(from_x, 2), 1 - zh]
        w_twin.append(post.send(line, line, twin))
    gain = gain_in[pl.ds(step, 1), :]
    for p in range(2):
        x_copies[p].wait_recv()

        @pl.loop(p * 4, p * 4 + 4, unroll=True)
        def norm(i):
            rows = pl.ds(pl.multiple_of(i * 16, 16), 16)
            value = z_sum(x_hi, rows) + x_got[rows, :].astype(F32)
            proj[rows, :] = value
            value = ratio_col[rows, :1] * value + looked[rows, :]
            scale = lax.rsqrt(jnp.mean(value * value, axis=1, keepdims=True) + 1e-06)
            x_rows[rows, :] = value
            scale_col[rows, :] = jnp.broadcast_to(scale, (16, 128))
            normed[rows, :] = (value * scale * gain).astype(BF)

    for copy in w_twin:
        copy.wait_recv()

    depth = normed.shape[1]
    for n in range(4):
        cols = slice(n * 512, (n + 1) * 512)
        head = w_full[:, :, :, :, :, :, cols].reshape(depth, 512)
        logits[:, cols] = jnp.dot(normed[...], head, preferred_element_type=F32)
    dr_col[...] = jnp.broadcast_to(target.astype(F32), (128, 128))

    @pl.loop(0, 8, unroll=2)
    def soft(i):
        rows = pl.ds(pl.multiple_of(i * 16, 16), 16)
        value = logits[rows, :]
        value = jnp.exp(value - jnp.max(value, axis=1, keepdims=True))
        share = value * (loss_weight / jnp.sum(value, axis=1, keepdims=True))
        hot = lax.broadcasted_iota(jnp.int32, (16, entries), 1) == dr_col[rows, :1].astype(
            jnp.int32
        )
        d_logit[rows, :] = (share - jnp.where(hot, loss_weight, 0.0)).astype(BF)

    for k in range(4):
        a, b = k // 2, (k % 2) * 2
        head = w_full[a, b : b + 2].reshape(256, entries)
        d_norm[:, k * 256 : (k + 1) * 256] = lax.dot_general(
            d_logit[...], head, NT, preferred_element_type=F32
        )

    @pl.loop(0, 8, unroll=4)
    def unnorm(i):
        rows = pl.ds(pl.multiple_of(i * 16, 16), 16)
        value, scale = x_rows[rows, :], scale_col[rows, :1]
        gated = gain * d_norm[rows, :]
        inner = jnp.mean(gated * value, axis=1, keepdims=True)
        d_x = scale * gated - value * (scale * scale * scale * inner)
        d_norm[rows, :] = d_x
        total = jnp.sum(d_x * proj[rows, :], axis=1, keepdims=True)
        dr_col[rows, :] = jnp.broadcast_to(total, (16, 128))

    for k in range(8):
        d_turn[k // 4, k % 4] = jnp.transpose(d_norm[:, k * 128 : (k + 1) * 128]).astype(BF)
    lane, far_lane = at128(quarter), at128(far_quarter)

    d_x_copies, d_z_copies = [], [[], [], [], []]
    for d in order:
        to_y = lax.rem(y + d, 4)
        d_x_copies.append(
            post.send(d_turn.at[:, to_y], d_all.at[step, :, to_y, :, lane], far)
        )

    def send_own(i):
        to_y = lax.rem(y + order[i], 4)
        for d in (2, 1, 3):
            d_z_copies[i].append(
                post.send(d_turn.at[:, to_y], d_all.at[step, :, to_y, :, lane], zs[d])
            )

    def send_far(i):
        to_y = lax.rem(y + order[i], 4)
        d_x_copies[i].wait_recv()
        view = d_all.at[step, :, to_y, :, far_lane]
        for d in (2, 1, 3):
            d_z_copies[i].append(post.send(view, view, zs[d]))

    send_own(0)
    send_own(1)
    small[...] = jnp.transpose(dr_col[...])[:8]
    small_copies = [post.send(small, small_all.at[hid], peer) for peer in hid_peers]
    for b in range(4):
        for a in range(2):
            d_all[step, a, b, :, lane] = d_turn[a, b]
    small_all[hid] = small[...]

    for k in range(8):
        cols = slice(k * 128, (k + 1) * 128)
        turned[cols, :] = jnp.transpose(normed[:, cols].astype(F32)).astype(BF)
    gp_swap = []

    def product_out(i):
        to_y = lax.rem(y + order[i], 4)
        for a in range(2):
            rows = at128(a * 4 + to_y)
            gp[a, to_y] = (
                jnp.dot(turned[rows, :], d_logit[...], preferred_element_type=F32)
                .astype(BF)
                .reshape(2, 2, 2, 16, entries)
            )
        gp_swap.append(post.send(gp.at[:, to_y, 1 - c], gp_c.at[:, to_y], twin))

    for i in range(4):
        product_out(i)
    send_far(0)
    send_own(2)
    send_far(1)
    send_own(3)

    def core_sum(a, b, e, f):
        return gp[a, b, c, e, f].astype(F32) + gp_c[a, b, e, f].astype(F32)

    ga_ys, gb_xs = [], []
    for i, d in enumerate(order[:3]):
        gp_swap[i].wait_recv()
        to_y = lax.rem(y + d, 4)
        for a in range(2):
            for e in range(2):
                ga_y[i, a, e] = core_sum(a, to_y, e, zh).astype(BF)
        ga_ys.append(post.send(ga_y.at[i], ga_yg.at[i], ys[d]))
    gp_swap[3].wait_recv()
    for i, d in enumerate(order[:3]):
        to_x = lax.rem(x + d, 4)
        for b in range(4):
            gb_x[i, b] = core_sum(lax.rem(to_x, 2), b, lax.div(to_x, 2), 1 - zh).astype(BF)
        gb_xs.append(post.send(gb_x.at[i], gb_xg.at[i], xs[d]))
    send_far(2)
    send_far(3)

    ip_ys = []

    def product_in(i):
        for copy in d_z_copies[i]:
            copy.wait_recv()
        to_y = lax.rem(y + order[i], 4)
        rows = [d_all[s, a, to_y] for s in range(2) for a in range(2)]
        product = jnp.dot(
            jnp.concatenate(rows, axis=0), scaled[...], preferred_element_type=F32
        ).astype(BF)
        for s in range(2):
            for a in range(2):
                for e in range(2):
                    start = (s * 2 + a) * 128 + e * 64
                    ip[s, a, to_y, e] = product[start : start + 64]
        return post.send(ip.at[:, :, to_y, 1 - c], ip_c.at[:, :, to_y], twin)

    def sum_in(i, swap):
        swap.wait_recv()
        to_y = lax.rem(y + order[i], 4)
        for s in range(2):
            for a in range(2):
                ip_y[i, s, a] = (
                    ip[s, a, to_y, c].astype(F32) + ip_c[s, a, to_y].astype(F32)
                ).astype(BF)
        ip_ys.append(post.send(ip_y.at[i], ip_yg.at[i], ys[order[i]]))

    swap = product_in(0)
    sum_in(0, swap)
    swap = product_in(1)
    sum_in(1, swap)
    for copy in ga_ys:
        copy.wait_recv()
    for a in range(2):
        for e in range(2):
            value = core_sum(a, y, e, zh)
            for i in range(3):
                value = value + ga_yg[i, a, e].astype(F32)
            ga_sum[a, e] = value.astype(BF)
    ga_xs = []
    for i, d in enumerate(order[:3]):
        to_x = lax.rem(x + d, 4)
        ga_xs.append(
            post.send(ga_sum.at[lax.rem(to_x, 2), lax.div(to_x, 2)], ga_xg.at[i], xs[d])
        )
    for copy in gb_xs:
        copy.wait_recv()
    for b in range(4):
        value = core_sum(x_lo, b, x_hi, 1 - zh)
        for i in range(3):
            value = value + gb_xg[i, b].astype(F32)
        gb_sum[b] = value.astype(BF)
    gb_ys = []
    for i, d in enumerate(order[:3]):
        gb_ys.append(post.send(gb_sum.at[lax.rem(y + d, 4)], gb_yg.at[i], ys[d]))
    swap = product_in(2)
    sum_in(2, swap)
    last_swap = product_in(3)

    for copy in gb_ys:
        copy.wait_recv()
    value = gb_sum[y].astype(F32)
    for i in range(3):
        value = value + gb_yg[i].astype(F32)
    gp_z[...] = value.astype(BF)
    gp_across = post.send(gp_z, gp_zg, zs[2])

    ratio_row = ratio_rows[0:1, :]
    for copy in small_copies:
        copy.wait_recv()
    for q in range(4):
        cols = slice(q * 128, (q + 1) * 128)
        r = ratio_rows[0:1, cols]
        total_dr = small_all[2 * q, 0:1, :] + small_all[2 * q + 1, 0:1, :]
        corr_col[cols, :] = column(r * r * r * total_dr * (1.0 / width_in))

    def back(k):
        cols = slice(k * 128, (k + 1) * 128)
        value = sum(
            jnp.dot(w_in[s, cols, :], d_all[s].reshape(depth, -1), preferred_element_type=F32)
            for s in range(2)
        )
        grad_hidden[:, cols] = (
            jnp.transpose(value * ratio_row)
            - corr_col[:, :1] * hidden[:, cols].astype(F32)
        ).astype(BF)

    back(0)
    back(1)
    for copy in ga_xs:
        copy.wait_recv()
    value = ga_sum[x_lo, x_hi].astype(F32)
    for i in range(3):
        value = value + ga_xg[i].astype(F32)
    gp_across.wait_recv()
    gp_rows[...] = value + gp_zg[...].astype(F32)
    theirs = gp_rows.at[pl.ds(pl.multiple_of((1 - step) * 8, 8), 8), :]
    gp_swap_rows = post.send(theirs, gp_pair, pair)
    last_swap.wait_recv()
    for copy in ip_ys:
        copy.wait_recv()

    def in_block(a, b):
        value = ip[a, b, y, c].astype(F32) + ip_c[a, b, y].astype(F32)
        for i in range(3):
            value = value + ip_yg[i, a, b].astype(F32)
        return value

    for a in range(2):
        ip_x[a] = in_block(a, 1 - x_lo).astype(BF)
    ip_beside = post.send(ip_x, ip_xg, beside)
    back(2)
    back(3)
    for a in range(2):
        grad_in[a] = in_block(a, x_lo)
    gp_swap_rows.wait_recv()
    grad_out[step] = gp_rows[pl.ds(pl.multiple_of(step * 8, 8), 8), :]
    grad_out[1 - step] = gp_pair[...]
    ip_beside.wait_recv()
    for a in range(2):
        grad_in[a] = grad_in[a] + ip_xg[a].astype(F32)
    post.close()


def finish(gh, gi, go, grad_hidden, grad_in, grad_out):
    grad_hidden[...] = gh[...]
    grad_in[...] = gi[...]
    grad_out[:, 0, :] = go[0]
    grad_out[:, 1, :] = go[1]


def shards(hidden, w_in, embedding, depth_gain, w_out, codebook_ids):
    hid_count = lax.axis_size("hid")
    seq_count = lax.axis_size("seq")
    width_in = hidden.shape[1] * hid_count
    depth = w_in.shape[2]
    entries = w_out.shape[2]
    frames, units = hidden.shape
    loss_weight = 2.0 * entries / (frames * seq_count)
    vmem = pl.BlockSpec(memory_space=pltpu.VMEM)
    anywhere = pl.BlockSpec(memory_space=pl.ANY)
    scratch = [
        ((frames, units), BF),
        ((2, units, depth), BF),
        ((entries, depth), BF),
        ((4, 2, 128, depth), BF),
        ((2, 128, depth), BF),
        ((2, 128, depth), BF),
        ((2, 2, 128, depth), BF),
        ((128, depth), BF),
        ((128, depth), BF),
        ((2, 8, entries), BF),
        ((4, 8, entries), BF),
        ((2, 4, 2, 2, 2, 16, entries), BF),
        ((8, 128), jnp.int32),
        ((2, 8, 128), jnp.int32),
        ((8, frames), F32),
        ((8, 8, frames), F32),
        ((8, frames), F32),
        ((128, 128), F32),
        ((frames, units), BF),
        ((128, depth), F32),
        ((128, depth), F32),
        ((128, depth), F32),
        ((128, depth), BF),
        ((depth, 128), BF),
        ((128, entries), F32),
        ((128, entries), BF),
        ((128, 128), F32),
        ((128, depth), F32),
        ((128, 128), F32),
        ((2, 4, 128, 128), BF),
        ((2, 2, 4, 128, frames), BF),
        ((8, 128), F32),
        ((8, 8, 128), F32),
        ((frames, 128), F32),
        ((2, 4, 2, 2, 2, 16, entries), BF),
        ((2, 4, 2, 2, 16, entries), BF),
        ((3, 2, 2, 16, entries), BF),
        ((3, 2, 2, 16, entries), BF),
        ((2, 2, 16, entries), BF),
        ((3, 16, entries), BF),
        ((3, 4, 16, entries), BF),
        ((3, 4, 16, entries), BF),
        ((4, 16, entries), BF),
        ((3, 16, entries), BF),
        ((16, entries), BF),
        ((16, entries), BF),
        ((16, entries), F32),
        ((8, entries), F32),
        ((2, 2, 4, 2, 64, units), BF),
        ((2, 2, 4, 64, units), BF),
        ((3, 2, 2, 64, units), BF),
        ((3, 2, 2, 64, units), BF),
        ((2, 64, units), BF),
        ((2, 64, units), BF),
    ]
    grad_hidden, grad_in, grad_out = pl.pallas_call(
        functools.partial(kernel, loss_weight, width_in),
        out_shape=[
            jax.ShapeDtypeStruct((frames, units), BF),
            jax.ShapeDtypeStruct((2, 64, units), F32),
            jax.ShapeDtypeStruct((2, 8, entries), F32),
        ],
        in_specs=[anywhere] * 3 + [vmem] * 3,
        out_specs=[vmem] * 3,
        scratch_shapes=[pltpu.VMEM(shape, dtype) for shape, dtype in scratch]
        + [
            pltpu.SemaphoreType.DMA((3,)),
            pltpu.SemaphoreType.DMA((112,)),
            pltpu.SemaphoreType.DMA((112,)),
        ],
        compiler_params=pltpu.CompilerParams(
            collective_id=0, has_side_effects=True, vmem_limit_bytes=60 * 1024 * 1024
        ),
        name="whole",
    )(hidden, w_in, embedding[0], depth_gain, w_out, codebook_ids)
    grad_hidden, grad_in, grad_out = pl.pallas_call(
        finish,
        out_shape=[
            jax.ShapeDtypeStruct((frames, units), BF),
            jax.ShapeDtypeStruct((2, 64, units), F32),
            jax.ShapeDtypeStruct((8, 2, entries), F32),
        ],
        in_specs=[vmem] * 3,
        out_specs=[vmem] * 3,
        name="finish",
    )(grad_hidden, grad_in, grad_out)
    return grad_hidden, jnp.transpose(grad_in, (0, 2, 1)), grad_out


def solution(mesh):
    placed = (
        P("seq", "hid"),
        P(None, "hid", None),
        P(),
        P(),
        P(("seq", "hid"), None, None),
        P(None, ("seq", "hid")),
    )
    return jax.shard_map(
        shards,
        mesh=mesh,
        in_specs=placed,
        out_specs=(P("seq", "hid"), P(None, "hid", "seq"), P(("seq", "hid"), None, None)),
        check_vma=False,
    )
```

time: 113 us -> 86.5 us (0.77)
  Pallas kernels: 104 us -> 85.7 us
  local copies, waits for them, and re-layouts: 8.22 us -> 0 us
    pallas_call x1, Pallas kernels: 104 us -> 83.6 us  [shards(): pl.pallas_call(functools.partial(kernel, loss_weight, width_in), out_shap...]
    unnamed x4 -> x0, local copies, waits for them, and re-layouts: 6.95 us -> none
    pallas_call x0 -> x1, Pallas kernels: none -> 2.07 us  [shards(): pl.pallas_call(finish, out_shape=[jax.ShapeDtypeStruct((frames, units), B...]
    pad x1 -> x0, local copies, waits for them, and re-layouts: 1.28 us -> none  [shards(): ids = jnp.pad(codebook_ids, ((0, 6), (0, 128 - own)))]
where the time goes in v3:
time: 86.5 us; the launch traced here: 86.4 us
  Pallas kernels  85.7 us (99%)
    pallas_call x1, Pallas kernels, shards(): pl.pallas_call(functools.partial(kernel, loss_weight, width_in), out_shap...  83.6 us
    pallas_call x1, Pallas kernels, shards(): pl.pallas_call(finish, out_shape=[jax.ShapeDtypeStruct((frames, units), B...  2.07 us

profile of v3, /device:TPU:0, one launch (start us, length us, event | category | flops | bytes accessed | tf_op | source)
XLA Modules:
  0.0 86.4 jit_solution(12791368710662037200)
XLA Ops:
  0.6 83.6 %whole.1 = (bf16[512,512]{1,0:T(8,128)(2,1)}, f32[2,64,512]{2,1,0:T(8,128)}, f32[2,8,2048]{2,1,0:T(8,128)}) custom-call(bf16[512,512]{1,0:T(8,128)(2,1)} %hidden_in.1, bf16[2,512,1024]{2,1,0:T(8,128)(2,1)} %w_in_in.1, bf16[2048,1024]{1,0:T(8,128)(2,1)} %bitcast.2, f32[2,1024]{1,0:T(2,128)} %gain_in.1, bf16[8,2,2048]{2,1,0:T(2,128)(2,1)} %w_out.1, s32[2,64]{1,0:T(2,128)} %ids.1), custom_call_target="tpu_custom_call" | custom-call | tf_op jit(solution)/shard_map/whole/pallas_call | solution.py:569
  84.3 2.1 %finish.1 = (bf16[512,512]{1,0:T(8,128)(2,1)}, f32[2,64,512]{2,1,0:T(8,128)}, f32[8,2,2048]{2,1,0:T(2,128)}) custom-call(bf16[512,512]{1,0:T(8,128)(2,1)} %get-tuple-element.9.gh, f32[2,64,512]{2,1,0:T(8,128)} %get-tuple-element.10.gi, f32[2,8,2048]{2,1,0:T(8,128)} %get-tuple-element.11.go), custom_call_target="tpu_custom_call" | custom-call | tf_op jit(solution)/shard_map/finish/pallas_call | solution.py:589

commit v4 on v3

--- a/solution.py
+++ b/solution.py
@@ -28,7 +28,7 @@
     barrier = pltpu.get_barrier_semaphore()
     for peer in peers:
         pl.semaphore_signal(barrier, inc=1, device_id=peer, device_id_type=MESH)
-    pl.semaphore_wait(barrier, len(peers))
+    return lambda: pl.semaphore_wait(barrier, len(peers))
 
 
 class Post:
@@ -69,13 +69,13 @@
         w_rows, w_got, w_full, ids_mine, ids_all,
         sq_mine, sq_all, ratio_rows, ratio_col, scaled, looked, x_rows, proj, normed, turned, logits,
         d_logit, scale_col, d_norm, dr_col, d_turn, d_all, small, small_all, corr_col,
-        gp, gp_c, ga_y, ga_yg, ga_sum, ga_xg, gb_x, gb_xg, gb_sum, gb_yg, gp_z, gp_zg, gp_rows, gp_pair,
-        ip, ip_c, ip_y, ip_yg, ip_x, ip_xg, local_sem, send_sem, recv_sem,
+        gp, gp_c, ga_y, ga_rel, ga_yg, ga_sum, ga_xg, gb_x, gb_rel, gb_xg, gb_sum, gb_yg,
+        gp_z, gp_zg, gp_rows, gp_pair, ip, ip_c, ip_y, ip_rel, ip_yg, ip_x, ip_xg, local_sem, send_sem, recv_sem,
     ) = rest[3:]
     x, y, z, c = place()
     x_lo, x_hi, step, zh = lax.rem(x, 2), lax.div(x, 2), lax.rem(z, 2), lax.div(z, 2)
     hid = x_hi * 4 + z
-    quarter, far_quarter = x_hi * 2 + zh, (1 - x_hi) * 2 + zh
+    quarter = x_hi * 2 + zh
     pair = device(x, y, z + 1 - 2 * step, c)
     far = device(x + 2, y, z, c)
     twin = device(x, y, z, c + 1)
@@ -86,26 +86,67 @@
     hid_peers = [device(x + dx, y, z + dz, c) for dz in (2, 1, 3, 0) for dx in (2, 0) if dx + dz]
     order = (2, 1, 3, 0)
 
+    sources = (
+        (hidden_in, hidden),
+        (w_in_in.at[step], w_in.at[step]),
+        (w_in_in.at[1 - step], w_in.at[1 - step]),
+        (embedding_in, embedding),
+    )
     loads = [
-        pltpu.make_async_copy(src, dst, local_sem.at[i])
-        for i, (src, dst) in enumerate(
-            ((hidden_in, hidden), (w_in_in, w_in), (embedding_in, embedding))
-        )
+        pltpu.make_async_copy(src, dst, local_sem.at[i]) for i, (src, dst) in enumerate(sources)
     ]
     for load in loads:
         load.start()
+    everyone_here = greet(hid_peers + [xs[1], xs[3]] + list(ys.values()) + [twin])
     w_rows[0] = w_out[:, 0, :]
     w_rows[1] = w_out[:, 1, :]
     ids_mine[...] = jnp.zeros_like(ids_mine)
     ids_mine[0:2, 0:64] = ids[...]
-    greet(hid_peers + [xs[1], xs[3]] + list(ys.values()) + [twin])
+    ids_all[step] = ids_mine[...]
+    w_got[z] = w_rows[step]
+
+    def chunk(dz):
+        to_z = lax.rem(z + dz, 4)
+        rows = [hidden[at128(fx * 2 + lax.div(to_z, 2)), :] for fx in range(2)]
+        product = jnp.dot(
+            jnp.concatenate(rows, axis=0), w_in[lax.rem(to_z, 2)], preferred_element_type=F32
+        ).astype(BF)
+        part[dz, 0] = product[:128]
+        part[dz, 1] = product[128:]
+
+    loads[0].wait()
+    loads[1].wait()
+    chunk(2)
+    everyone_here()
     post = Post(send_sem, recv_sem)
+
+    bounds = ((0, 64), (64, 96), (96, 128))
+    pieces = [pl.ds(a, b - a) for a, b in bounds]
+    relays, z_copies = [[] for _ in pieces], [[] for _ in pieces]
+
+    def send_opposite(p):
+        rows = pieces[p]
+        relays[p].append(post.send(part.at[2, 0, rows], relay.at[0, rows], zs[1]))
+        relays[p].append(post.send(part.at[2, 1, rows], relay.at[1, rows], zs[3]))
+
+    def send_direct(p, dz):
+        rows, fx, slot = pieces[p], (1 if dz == 1 else 0), (0 if dz == 1 else 1)
+        z_copies[p].append(post.send(part.at[dz, fx, rows], z_got.at[slot, fx, rows], zs[dz]))
+
+    def send_sums(p):
+        for fx, dz in ((0, 1), (1, 3)):
+            rows = pieces[p]
+            relays[p][fx].wait_recv()
+            relay_sum[fx, rows, :] = (
+                part[dz, fx, rows, :].astype(F32) + relay[fx, rows, :].astype(F32)
+            ).astype(BF)
+            z_copies[p].append(
+                post.send(relay_sum.at[fx, rows], z_got.at[fx, fx, rows], zs[dz])
+            )
 
     w_z = [post.send(w_rows.at[(step + d) % 2], w_got.at[z], zs[d]) for d in (2, 1, 3)]
     ids_swap = post.send(ids_mine, ids_all.at[step], pair)
-    ids_all[step] = ids_mine[...]
-    w_got[z] = w_rows[step]
-    loads[0].wait()
+    send_opposite(0)
     h = hidden[...].astype(F32)
     h2 = h * h
     top = h2.astype(BF)
@@ -115,50 +156,16 @@
         ones, low, NT, preferred_element_type=F32
     )
     sq_all[hid] = sq_mine[...]
-    loads[1].wait()
-
-    def chunk(dz):
-        to_z = lax.rem(z + dz, 4)
-        rows = [hidden[at128(fx * 2 + lax.div(to_z, 2)), :] for fx in range(2)]
-        product = jnp.dot(
-            jnp.concatenate(rows, axis=0), w_in[lax.rem(to_z, 2)], preferred_element_type=F32
-        ).astype(BF)
-        part[dz, 0] = product[:128]
-        part[dz, 1] = product[128:]
-
-    halves = (pl.ds(0, 64), pl.ds(64, 64))
-    relays, z_copies = [[], []], [[], []]
-
-    def send_opposite(p):
-        rows = halves[p]
-        relays[p].append(post.send(part.at[2, 0, rows], relay.at[0, rows], zs[1]))
-        relays[p].append(post.send(part.at[2, 1, rows], relay.at[1, rows], zs[3]))
-
-    def send_direct(p, dz):
-        rows, fx, slot = halves[p], (1 if dz == 1 else 0), (0 if dz == 1 else 1)
-        z_copies[p].append(post.send(part.at[dz, fx, rows], z_got.at[slot, fx, rows], zs[dz]))
-
-    def send_sums(p):
-        for fx, dz in ((0, 1), (1, 3)):
-            rows = halves[p]
-            relays[p][fx].wait_recv()
-            relay_sum[fx, rows, :] = (
-                part[dz, fx, rows, :].astype(F32) + relay[fx, rows, :].astype(F32)
-            ).astype(BF)
-            z_copies[p].append(
-                post.send(relay_sum.at[fx, rows], z_got.at[fx, fx, rows], zs[dz])
-            )
-
-    chunk(2)
-    send_opposite(0)
-    sq_copies = [post.send(sq_mine, sq_all.at[hid], peer) for peer in hid_peers]
+    loads[2].wait()
     chunk(1)
     send_direct(0, 1)
+    sq_copies = [post.send(sq_mine, sq_all.at[hid], peer) for peer in hid_peers]
     chunk(3)
     send_direct(0, 3)
-    send_opposite(1)
-    send_direct(1, 1)
-    send_direct(1, 3)
+    for p in (1, 2):
+        send_opposite(p)
+        send_direct(p, 1)
+        send_direct(p, 3)
     for copy in w_z:
         copy.wait_recv()
     for e in range(2):
@@ -181,6 +188,7 @@
     wb_x = {d: post.send(line, line, xs[d]) for d in (2, 1, 3)}
     w_twin.append(post.send(line, line, twin))
     send_sums(1)
+    send_sums(2)
 
     for copy in sq_copies:
         copy.wait_recv()
@@ -204,7 +212,7 @@
     target = jnp.where(step == 1, current, previous)
     entries = logits.shape[1]
     lanes = lax.broadcasted_iota(jnp.int32, (128, entries), 1)
-    loads[2].wait()
+    loads[3].wait()
     pick = jnp.where(lanes == previous, 1.0, 0.0).astype(BF)
     live = step.astype(F32)
     for n in range(2):
@@ -219,16 +227,16 @@
         )
 
     x_copies = []
-    for p in range(2):
+    for p in range(3):
         for copy in z_copies[p]:
             copy.wait_recv()
 
-        @pl.loop(p * 4, p * 4 + 4, unroll=True)
+        @pl.loop(bounds[p][0] // 16, bounds[p][1] // 16, unroll=True)
         def to_far(i):
             rows = pl.ds(pl.multiple_of(i * 16, 16), 16)
             x_send[rows, :] = z_sum(1 - x_hi, rows).astype(BF)
 
-        x_copies.append(post.send(x_send.at[halves[p]], x_got.at[halves[p]], far))
+        x_copies.append(post.send(x_send.at[pieces[p]], x_got.at[pieces[p]], far))
     for d in (1, 3, 2):
         wa_y[d].wait_recv()
         line = w_full.at[:, lax.rem(y + 4 - d, 4), c, :, zh]
@@ -239,10 +247,10 @@
         line = w_full.at[lax.rem(from_x, 2), :, c, lax.div(from_x, 2), 1 - zh]
         w_twin.append(post.send(line, line, twin))
     gain = gain_in[pl.ds(step, 1), :]
-    for p in range(2):
+    for p in range(3):
         x_copies[p].wait_recv()
 
-        @pl.loop(p * 4, p * 4 + 4, unroll=True)
+        @pl.loop(bounds[p][0] // 16, bounds[p][1] // 16, unroll=True)
         def norm(i):
             rows = pl.ds(pl.multiple_of(i * 16, 16), 16)
             value = z_sum(x_hi, rows) + x_got[rows, :].astype(F32)
@@ -294,31 +302,41 @@
 
     for k in range(8):
         d_turn[k // 4, k % 4] = jnp.transpose(d_norm[:, k * 128 : (k + 1) * 128]).astype(BF)
-    lane, far_lane = at128(quarter), at128(far_quarter)
-
-    d_x_copies, d_z_copies = [], [[], [], [], []]
+    lane = at128(quarter)
+
+    def lane_of(fx, dz):
+        return at128(fx * 2 + lax.div(lax.rem(z + dz, 4), 2))
+
+    d_x_copies = []
     for d in order:
         to_y = lax.rem(y + d, 4)
         d_x_copies.append(
             post.send(d_turn.at[:, to_y], d_all.at[step, :, to_y, :, lane], far)
         )
+    first_hop, second_hop = {}, [[], [], [], []]
 
     def send_own(i):
         to_y = lax.rem(y + order[i], 4)
-        for d in (2, 1, 3):
-            d_z_copies[i].append(
-                post.send(d_turn.at[:, to_y], d_all.at[step, :, to_y, :, lane], zs[d])
-            )
+        view = d_all.at[step, :, to_y, :, lane]
+        first_hop[i, 0] = [post.send(d_turn.at[:, to_y], view, zs[d]) for d in (1, 3)]
 
     def send_far(i):
         to_y = lax.rem(y + order[i], 4)
         d_x_copies[i].wait_recv()
-        view = d_all.at[step, :, to_y, :, far_lane]
-        for d in (2, 1, 3):
-            d_z_copies[i].append(post.send(view, view, zs[d]))
+        view = d_all.at[step, :, to_y, :, lane_of(1 - x_hi, 0)]
+        first_hop[i, 1] = [post.send(view, view, zs[d]) for d in (1, 3)]
+
+    def forward(i, other):
+        to_y = lax.rem(y + order[i], 4)
+        fx = 1 - x_hi if other else x_hi
+        for a, (dz, copy) in enumerate(zip((3, 1), first_hop[i, other])):
+            copy.wait_recv()
+            view = d_all.at[1 - step, a, to_y, :, lane_of(fx, dz)]
+            second_hop[i].append(post.send(view, view, zs[4 - dz]))
 
     send_own(0)
     send_own(1)
+    send_own(2)
     small[...] = jnp.transpose(dr_col[...])[:8]
     small_copies = [post.send(small, small_all.at[hid], peer) for peer in hid_peers]
     for b in range(4):
@@ -344,35 +362,63 @@
 
     for i in range(4):
         product_out(i)
-    send_far(0)
-    send_own(2)
-    send_far(1)
-    send_own(3)
-
     def core_sum(a, b, e, f):
         return gp[a, b, c, e, f].astype(F32) + gp_c[a, b, e, f].astype(F32)
 
-    ga_ys, gb_xs = [], []
-    for i, d in enumerate(order[:3]):
-        gp_swap[i].wait_recv()
-        to_y = lax.rem(y + d, 4)
-        for a in range(2):
-            for e in range(2):
-                ga_y[i, a, e] = core_sum(a, to_y, e, zh).astype(BF)
-        ga_ys.append(post.send(ga_y.at[i], ga_yg.at[i], ys[d]))
+    def ga_part(i, a, more=None):
+        to_y = lax.rem(y + order[i], 4)
+        for e in range(2):
+            value = core_sum(a, to_y, e, zh)
+            if more is not None:
+                value = value + ga_rel[more, e].astype(F32)
+            ga_y[i, a, e] = value.astype(BF)
+        return ga_y.at[i, a]
+
+    def gb_part(i, k, more=None):
+        to_x = lax.rem(x + order[i], 4)
+        for b in range(2):
+            value = core_sum(lax.rem(to_x, 2), 2 * k + b, lax.div(to_x, 2), 1 - zh)
+            if more is not None:
+                value = value + gb_rel[more, b].astype(F32)
+            gb_x[i, k, b] = value.astype(BF)
+        return gb_x.at[i, k]
+
+    gp_swap[0].wait_recv()
+    ga_relay = [post.send(ga_part(0, a), ga_rel.at[a], ys[d]) for a, d in ((0, 1), (1, 3))]
+    gp_swap[1].wait_recv()
+    ga_ys = [post.send(ga_part(1, 1), ga_yg.at[0, 1], ys[1])]
+    gp_swap[2].wait_recv()
+    ga_ys.append(post.send(ga_part(2, 0), ga_yg.at[1, 0], ys[3]))
     gp_swap[3].wait_recv()
-    for i, d in enumerate(order[:3]):
-        to_x = lax.rem(x + d, 4)
-        for b in range(4):
-            gb_x[i, b] = core_sum(lax.rem(to_x, 2), b, lax.div(to_x, 2), 1 - zh).astype(BF)
-        gb_xs.append(post.send(gb_x.at[i], gb_xg.at[i], xs[d]))
+    gb_relay = [post.send(gb_part(0, k), gb_rel.at[k], xs[d]) for k, d in ((0, 1), (1, 3))]
+    gb_xs = [
+        post.send(gb_part(1, 1), gb_xg.at[0, 1], xs[1]),
+        post.send(gb_part(2, 0), gb_xg.at[1, 0], xs[3]),
+    ]
+    forward(0, 0)
+    send_far(0)
+    forward(1, 0)
+    send_own(3)
+    send_far(1)
+    forward(2, 0)
+    ga_relay[0].wait_recv()
+    ga_ys.append(post.send(ga_part(1, 0, 0), ga_yg.at[0, 0], ys[1]))
+    ga_relay[1].wait_recv()
+    ga_ys.append(post.send(ga_part(2, 1, 1), ga_yg.at[1, 1], ys[3]))
     send_far(2)
+    forward(0, 1)
+    gb_relay[0].wait_recv()
+    gb_xs.append(post.send(gb_part(1, 0, 0), gb_xg.at[0, 0], xs[1]))
+    gb_relay[1].wait_recv()
+    gb_xs.append(post.send(gb_part(2, 1, 1), gb_xg.at[1, 1], xs[3]))
+    forward(3, 0)
     send_far(3)
-
-    ip_ys = []
+    forward(1, 1)
+
+    ip_ys, ip_relay = [], []
 
     def product_in(i):
-        for copy in d_z_copies[i]:
+        for copy in second_hop[i]:
             copy.wait_recv()
         to_y = lax.rem(y + order[i], 4)
         rows = [d_all[s, a, to_y] for s in range(2) for a in range(2)]
@@ -389,23 +435,32 @@
     def sum_in(i, swap):
         swap.wait_recv()
         to_y = lax.rem(y + order[i], 4)
+        if i:
+            ip_relay[i - 1].wait_recv()
         for s in range(2):
             for a in range(2):
-                ip_y[i, s, a] = (
-                    ip[s, a, to_y, c].astype(F32) + ip_c[s, a, to_y].astype(F32)
-                ).astype(BF)
-        ip_ys.append(post.send(ip_y.at[i], ip_yg.at[i], ys[order[i]]))
+                value = ip[s, a, to_y, c].astype(F32) + ip_c[s, a, to_y].astype(F32)
+                if s == i - 1:
+                    value = value + ip_rel[s, a].astype(F32)
+                ip_y[i, s, a] = value.astype(BF)
+        if i:
+            ip_ys.append(post.send(ip_y.at[i], ip_yg.at[i - 1], ys[order[i]]))
+        else:
+            for s, d in ((0, 1), (1, 3)):
+                ip_relay.append(post.send(ip_y.at[0, s], ip_rel.at[s], ys[d]))
 
     swap = product_in(0)
     sum_in(0, swap)
+    forward(2, 1)
     swap = product_in(1)
     sum_in(1, swap)
+    forward(3, 1)
     for copy in ga_ys:
         copy.wait_recv()
     for a in range(2):
         for e in range(2):
             value = core_sum(a, y, e, zh)
-            for i in range(3):
+            for i in range(2):
                 value = value + ga_yg[i, a, e].astype(F32)
             ga_sum[a, e] = value.astype(BF)
     ga_xs = []
@@ -418,8 +473,8 @@
         copy.wait_recv()
     for b in range(4):
         value = core_sum(x_lo, b, x_hi, 1 - zh)
-        for i in range(3):
-            value = value + gb_xg[i, b].astype(F32)
+        for i in range(2):
+            value = value + gb_xg[i, b // 2, b % 2].astype(F32)
         gb_sum[b] = value.astype(BF)
     gb_ys = []
     for i, d in enumerate(order[:3]):
@@ -473,7 +528,7 @@
 
     def in_block(a, b):
         value = ip[a, b, y, c].astype(F32) + ip_c[a, b, y].astype(F32)
-        for i in range(3):
+        for i in range(2):
             value = value + ip_yg[i, a, b].astype(F32)
         return value
 
@@ -548,11 +603,13 @@
         ((2, 4, 2, 2, 2, 16, entries), BF),
         ((2, 4, 2, 2, 16, entries), BF),
         ((3, 2, 2, 16, entries), BF),
+        ((2, 2, 16, entries), BF),
+        ((2, 2, 2, 16, entries), BF),
+        ((2, 2, 16, entries), BF),
+        ((3, 16, entries), BF),
         ((3, 2, 2, 16, entries), BF),
         ((2, 2, 16, entries), BF),
-        ((3, 16, entries), BF),
-        ((3, 4, 16, entries), BF),
-        ((3, 4, 16, entries), BF),
+        ((2, 2, 2, 16, entries), BF),
         ((4, 16, entries), BF),
         ((3, 16, entries), BF),
         ((16, entries), BF),
@@ -562,7 +619,8 @@
         ((2, 2, 4, 2, 64, units), BF),
         ((2, 2, 4, 64, units), BF),
         ((3, 2, 2, 64, units), BF),
-        ((3, 2, 2, 64, units), BF),
+        ((2, 2, 64, units), BF),
+        ((2, 2, 2, 64, units), BF),
         ((2, 64, units), BF),
         ((2, 64, units), BF),
     ]
@@ -577,9 +635,9 @@
         out_specs=[vmem] * 3,
         scratch_shapes=[pltpu.VMEM(shape, dtype) for shape, dtype in scratch]
         + [
-            pltpu.SemaphoreType.DMA((3,)),
-            pltpu.SemaphoreType.DMA((112,)),
-            pltpu.SemaphoreType.DMA((112,)),
+            pltpu.SemaphoreType.DMA((4,)),
+            pltpu.SemaphoreType.DMA((144,)),
+            pltpu.SemaphoreType.DMA((144,)),
         ],
         compiler_params=pltpu.CompilerParams(
             collective_id=0, has_side_effects=True, vmem_limit_bytes=60 * 1024 * 1024

time: 86.5 us -> 89.4 us (1.034)
  Pallas kernels: 85.7 us -> 88.6 us
    pallas_call x1, Pallas kernels: 83.6 us -> 86.5 us  [shards(): pl.pallas_call(functools.partial(kernel, loss_weight, width_in), out_shap...]
where the time goes in v4:
time: 89.4 us; the launch traced here: 89.3 us
  Pallas kernels  88.6 us (99%)
    pallas_call x1, Pallas kernels, shards(): pl.pallas_call(functools.partial(kernel, loss_weight, width_in), out_shap...  86.5 us
    pallas_call x1, Pallas kernels, shards(): pl.pallas_call(finish, out_shape=[jax.ShapeDtypeStruct((frames, units), B...  2.07 us

profile of v4, /device:TPU:0, one launch (start us, length us, event | category | flops | bytes accessed | tf_op | source)
XLA Modules:
  0.0 89.3 jit_solution(17067365062027306226)
XLA Ops:
  0.6 86.5 %whole.1 = (bf16[512,512]{1,0:T(8,128)(2,1)}, f32[2,64,512]{2,1,0:T(8,128)}, f32[2,8,2048]{2,1,0:T(8,128)}) custom-call(bf16[512,512]{1,0:T(8,128)(2,1)} %hidden_in.1, bf16[2,512,1024]{2,1,0:T(8,128)(2,1)} %w_in_in.1, bf16[2048,1024]{1,0:T(8,128)(2,1)} %bitcast.2, f32[2,1024]{1,0:T(2,128)} %gain_in.1, bf16[8,2,2048]{2,1,0:T(2,128)(2,1)} %w_out.1, s32[2,64]{1,0:T(2,128)} %ids.1), custom_call_target="tpu_custom_call" | custom-call | tf_op jit(solution)/shard_map/whole/pallas_call | solution.py:627
  87.2 2.1 %finish.1 = (bf16[512,512]{1,0:T(8,128)(2,1)}, f32[2,64,512]{2,1,0:T(8,128)}, f32[8,2,2048]{2,1,0:T(2,128)}) custom-call(bf16[512,512]{1,0:T(8,128)(2,1)} %get-tuple-element.9.gh, f32[2,64,512]{2,1,0:T(8,128)} %get-tuple-element.10.gi, f32[2,8,2048]{2,1,0:T(8,128)} %get-tuple-element.11.go), custom_call_target="tpu_custom_call" | custom-call | tf_op jit(solution)/shard_map/finish/pallas_call | solution.py:647

commit v5 on v4

--- a/solution.py
+++ b/solution.py
@@ -302,41 +302,29 @@
 
     for k in range(8):
         d_turn[k // 4, k % 4] = jnp.transpose(d_norm[:, k * 128 : (k + 1) * 128]).astype(BF)
-    lane = at128(quarter)
-
-    def lane_of(fx, dz):
-        return at128(fx * 2 + lax.div(lax.rem(z + dz, 4), 2))
-
-    d_x_copies = []
-    for d in order:
-        to_y = lax.rem(y + d, 4)
-        d_x_copies.append(
-            post.send(d_turn.at[:, to_y], d_all.at[step, :, to_y, :, lane], far)
-        )
-    first_hop, second_hop = {}, [[], [], [], []]
-
-    def send_own(i):
-        to_y = lax.rem(y + order[i], 4)
-        view = d_all.at[step, :, to_y, :, lane]
-        first_hop[i, 0] = [post.send(d_turn.at[:, to_y], view, zs[d]) for d in (1, 3)]
-
-    def send_far(i):
-        to_y = lax.rem(y + order[i], 4)
-        d_x_copies[i].wait_recv()
-        view = d_all.at[step, :, to_y, :, lane_of(1 - x_hi, 0)]
-        first_hop[i, 1] = [post.send(view, view, zs[d]) for d in (1, 3)]
-
-    def forward(i, other):
-        to_y = lax.rem(y + order[i], 4)
-        fx = 1 - x_hi if other else x_hi
-        for a, (dz, copy) in enumerate(zip((3, 1), first_hop[i, other])):
-            copy.wait_recv()
-            view = d_all.at[1 - step, a, to_y, :, lane_of(fx, dz)]
-            second_hop[i].append(post.send(view, view, zs[4 - dz]))
-
-    send_own(0)
-    send_own(1)
-    send_own(2)
+    lane, far_lane = at128(quarter), at128((1 - x_hi) * 2 + zh)
+
+    def piece(k):
+        return (1 - x_lo if k < 4 else x_lo), lax.rem(y + order[k % 4], 4)
+
+    d_x_copies, d_z_copies = [], [[] for _ in range(8)]
+    for k in range(8):
+        b, to_y = piece(k)
+        d_x_copies.append(post.send(d_turn.at[b, to_y], d_all.at[step, b, to_y, :, lane], far))
+
+    def send_own(k):
+        b, to_y = piece(k)
+        view = d_all.at[step, b, to_y, :, lane]
+        d_z_copies[k] += [post.send(d_turn.at[b, to_y], view, zs[d]) for d in (2, 1, 3)]
+
+    def send_far(k):
+        b, to_y = piece(k)
+        d_x_copies[k].wait_recv()
+        view = d_all.at[step, b, to_y, :, far_lane]
+        d_z_copies[k] += [post.send(view, view, zs[d]) for d in (2, 1, 3)]
+
+    for k in range(3):
+        send_own(k)
     small[...] = jnp.transpose(dr_col[...])[:8]
     small_copies = [post.send(small, small_all.at[hid], peer) for peer in hid_peers]
     for b in range(4):
@@ -395,66 +383,62 @@
         post.send(gb_part(1, 1), gb_xg.at[0, 1], xs[1]),
         post.send(gb_part(2, 0), gb_xg.at[1, 0], xs[3]),
     ]
-    forward(0, 0)
-    send_far(0)
-    forward(1, 0)
-    send_own(3)
-    send_far(1)
-    forward(2, 0)
+    for k in range(8):
+        send_far(k)
+        if k < 5:
+            send_own(k + 3)
     ga_relay[0].wait_recv()
     ga_ys.append(post.send(ga_part(1, 0, 0), ga_yg.at[0, 0], ys[1]))
     ga_relay[1].wait_recv()
     ga_ys.append(post.send(ga_part(2, 1, 1), ga_yg.at[1, 1], ys[3]))
-    send_far(2)
-    forward(0, 1)
+
+    ip_ys, ip_relay = [[], []], [[], []]
+
+    def grad_in_piece(k):
+        for copy in d_z_copies[k]:
+            copy.wait_recv()
+        b, to_y = piece(k)
+        late, i = k // 4, k % 4
+        rows = [d_all[s, b, to_y] for s in range(2)]
+        product = jnp.dot(
+            jnp.concatenate(rows, axis=0), scaled[...], preferred_element_type=F32
+        ).astype(BF)
+        for s in range(2):
+            for e in range(2):
+                start = s * 128 + e * 64
+                ip[late, to_y, e, s] = product[start : start + 64]
+        swap = post.send(ip.at[late, to_y, 1 - c], ip_c.at[late, to_y], twin)
+        swap.wait_recv()
+        if i == 3:
+            return
+        if i:
+            ip_relay[late][i - 1].wait_recv()
+        for s in range(2):
+            value = ip[late, to_y, c, s].astype(F32) + ip_c[late, to_y, s].astype(F32)
+            if s == i - 1:
+                value = value + ip_rel[late, s].astype(F32)
+            ip_y[late, i, s] = value.astype(BF)
+        if i:
+            ip_ys[late].append(
+                post.send(ip_y.at[late, i], ip_yg.at[late, i - 1], ys[order[i]])
+            )
+        else:
+            for s, d in ((0, 1), (1, 3)):
+                ip_relay[late].append(post.send(ip_y.at[late, 0, s], ip_rel.at[late, s], ys[d]))
+
+    def in_block(late, s):
+        value = ip[late, y, c, s].astype(F32) + ip_c[late, y, s].astype(F32)
+        for i in range(2):
+            value = value + ip_yg[late, i, s].astype(F32)
+        return value
+
+    grad_in_piece(0)
     gb_relay[0].wait_recv()
     gb_xs.append(post.send(gb_part(1, 0, 0), gb_xg.at[0, 0], xs[1]))
     gb_relay[1].wait_recv()
     gb_xs.append(post.send(gb_part(2, 1, 1), gb_xg.at[1, 1], xs[3]))
-    forward(3, 0)
-    send_far(3)
-    forward(1, 1)
-
-    ip_ys, ip_relay = [], []
-
-    def product_in(i):
-        for copy in second_hop[i]:
-            copy.wait_recv()
-        to_y = lax.rem(y + order[i], 4)
-        rows = [d_all[s, a, to_y] for s in range(2) for a in range(2)]
-        product = jnp.dot(
-            jnp.concatenate(rows, axis=0), scaled[...], preferred_element_type=F32
-        ).astype(BF)
-        for s in range(2):
-            for a in range(2):
-                for e in range(2):
-                    start = (s * 2 + a) * 128 + e * 64
-                    ip[s, a, to_y, e] = product[start : start + 64]
-        return post.send(ip.at[:, :, to_y, 1 - c], ip_c.at[:, :, to_y], twin)
-
-    def sum_in(i, swap):
-        swap.wait_recv()
-        to_y = lax.rem(y + order[i], 4)
-        if i:
-            ip_relay[i - 1].wait_recv()
-        for s in range(2):
-            for a in range(2):
-                value = ip[s, a, to_y, c].astype(F32) + ip_c[s, a, to_y].astype(F32)
-                if s == i - 1:
-                    value = value + ip_rel[s, a].astype(F32)
-                ip_y[i, s, a] = value.astype(BF)
-        if i:
-            ip_ys.append(post.send(ip_y.at[i], ip_yg.at[i - 1], ys[order[i]]))
-        else:
-            for s, d in ((0, 1), (1, 3)):
-                ip_relay.append(post.send(ip_y.at[0, s], ip_rel.at[s], ys[d]))
-
-    swap = product_in(0)
-    sum_in(0, swap)
-    forward(2, 1)
-    swap = product_in(1)
-    sum_in(1, swap)
-    forward(3, 1)
+    grad_in_piece(1)
+    grad_in_piece(2)
     for copy in ga_ys:
         copy.wait_recv()
     for a in range(2):
@@ -479,10 +463,14 @@
     gb_ys = []
     for i, d in enumerate(order[:3]):
         gb_ys.append(post.send(gb_sum.at[lax.rem(y + d, 4)], gb_yg.at[i], ys[d]))
-    swap = product_in(2)
-    sum_in(2, swap)
-    last_swap = product_in(3)
-
+    grad_in_piece(3)
+    grad_in_piece(4)
+    for copy in ip_ys[0]:
+        copy.wait_recv()
+    for s in range(2):
+        ip_x[s] = in_block(0, s).astype(BF)
+    ip_beside = post.send(ip_x, ip_xg, beside)
+    grad_in_piece(5)
     for copy in gb_ys:
         copy.wait_recv()
     value = gb_sum[y].astype(F32)
@@ -490,6 +478,14 @@
         value = value + gb_yg[i].astype(F32)
     gp_z[...] = value.astype(BF)
     gp_across = post.send(gp_z, gp_zg, zs[2])
+    grad_in_piece(6)
+    for copy in ga_xs:
+        copy.wait_recv()
+    value = ga_sum[x_lo, x_hi].astype(F32)
+    for i in range(3):
+        value = value + ga_xg[i].astype(F32)
+    gp_rows[...] = value
+    grad_in_piece(7)
 
     ratio_row = ratio_rows[0:1, :]
     for copy in small_copies:
@@ -513,38 +509,20 @@
 
     back(0)
     back(1)
-    for copy in ga_xs:
-        copy.wait_recv()
-    value = ga_sum[x_lo, x_hi].astype(F32)
-    for i in range(3):
-        value = value + ga_xg[i].astype(F32)
     gp_across.wait_recv()
-    gp_rows[...] = value + gp_zg[...].astype(F32)
+    gp_rows[...] = gp_rows[...] + gp_zg[...].astype(F32)
     theirs = gp_rows.at[pl.ds(pl.multiple_of((1 - step) * 8, 8), 8), :]
     gp_swap_rows = post.send(theirs, gp_pair, pair)
-    last_swap.wait_recv()
-    for copy in ip_ys:
-        copy.wait_recv()
-
-    def in_block(a, b):
-        value = ip[a, b, y, c].astype(F32) + ip_c[a, b, y].astype(F32)
-        for i in range(2):
-            value = value + ip_yg[i, a, b].astype(F32)
-        return value
-
-    for a in range(2):
-        ip_x[a] = in_block(a, 1 - x_lo).astype(BF)
-    ip_beside = post.send(ip_x, ip_xg, beside)
     back(2)
     back(3)
-    for a in range(2):
-        grad_in[a] = in_block(a, x_lo)
+    ip_beside.wait_recv()
+    for copy in ip_ys[1]:
+        copy.wait_recv()
+    for s in range(2):
+        grad_in[s] = in_block(1, s) + ip_xg[s].astype(F32)
     gp_swap_rows.wait_recv()
     grad_out[step] = gp_rows[pl.ds(pl.multiple_of(step * 8, 8), 8), :]
     grad_out[1 - step] = gp_pair[...]
-    ip_beside.wait_recv()
-    for a in range(2):
-        grad_in[a] = grad_in[a] + ip_xg[a].astype(F32)
     post.close()
 
 
@@ -616,9 +594,9 @@
         ((16, entries), BF),
         ((16, entries), F32),
         ((8, entries), F32),
-        ((2, 2, 4, 2, 64, units), BF),
-        ((2, 2, 4, 64, units), BF),
-        ((3, 2, 2, 64, units), BF),
+        ((2, 4, 2, 2, 64, units), BF),
+        ((2, 4, 2, 64, units), BF),
+        ((2, 3, 2, 64, units), BF),
         ((2, 2, 64, units), BF),
         ((2, 2, 2, 64, units), BF),
         ((2, 64, units), BF),
@@ -636,11 +614,11 @@
         scratch_shapes=[pltpu.VMEM(shape, dtype) for shape, dtype in scratch]
         + [
             pltpu.SemaphoreType.DMA((4,)),
-            pltpu.SemaphoreType.DMA((144,)),
-            pltpu.SemaphoreType.DMA((144,)),
+            pltpu.SemaphoreType.DMA((176,)),
+            pltpu.SemaphoreType.DMA((176,)),
         ],
         compiler_params=pltpu.CompilerParams(
-            collective_id=0, has_side_effects=True, vmem_limit_bytes=60 * 1024 * 1024
+            collective_id=0, has_side_effects=True, vmem_limit_bytes=62 * 1024 * 1024
         ),
         name="whole",
     )(hidden, w_in, embedding[0], depth_gain, w_out, codebook_ids)
@@ -653,6 +631,7 @@
         ],
         in_specs=[vmem] * 3,
         out_specs=[vmem] * 3,
+        compiler_params=pltpu.CompilerParams(vmem_limit_bytes=4 * 1024 * 1024),
         name="finish",
     )(grad_hidden, grad_in, grad_out)
     return grad_hidden, jnp.transpose(grad_in, (0, 2, 1)), grad_out

time: 89.4 us -> 81.7 us (0.914)
  Pallas kernels: 88.6 us -> 77.9 us
  local copies, waits for them, and re-layouts: 0 us -> 2.89 us
    pallas_call x1, Pallas kernels: 86.5 us -> 77 us  [shards(): pl.pallas_call(functools.partial(kernel, loss_weight, width_in), out_shap...]
    unnamed x0 -> x6, local copies, waits for them, and re-layouts: none -> 2.89 us
    pallas_call x1, Pallas kernels: 2.07 us -> 0.97 us  [shards(): pl.pallas_call(finish, out_shape=[jax.ShapeDtypeStruct((frames, units), B...]
where the time goes in v5:
time: 81.7 us; the launch traced here: 81.5 us
  Pallas kernels  77.9 us (95%)
  local copies, waits for them, and re-layouts  2.89 us (4%)
    pallas_call x1, Pallas kernels, shards(): pl.pallas_call(functools.partial(kernel, loss_weight, width_in), out_shap...  77 us
    unnamed x6, local copies, waits for them, and re-layouts  2.89 us

profile of v5, /device:TPU:0, one launch (start us, length us, event | category | flops | bytes accessed | tf_op | source)
XLA Modules:
  0.0 81.5 jit_solution(16451671016921228830)
XLA Ops:
  0.6 77.0 %whole.1 = (bf16[512,512]{1,0:T(8,128)(2,1)}, f32[2,64,512]{2,1,0:T(8,128)}, f32[2,8,2048]{2,1,0:T(8,128)}) custom-call(bf16[512,512]{1,0:T(8,128)(2,1)} %hidden_in.1, bf16[2,512,1024]{2,1,0:T(8,128)(2,1)} %w_in_in.1, bf16[2048,1024]{1,0:T(8,128)(2,1)} %bitcast.2, f32[2,1024]{1,0:T(2,128)} %gain_in.1, bf16[8,2,2048]{2,1,0:T(2,128)(2,1)} %w_out.1, s32[2,64]{1,0:T(2,128)} %ids.1), custom_call_target="tpu_custom_call" | custom-call | tf_op jit(solution)/shard_map/whole/pallas_call | solution.py:605
  77.6 0.0 copy-start
  77.6 1.0 %copy-done = bf16[512,512]{1,0:T(8,128)(2,1)S(1)} copy-done((bf16[512,512]{1,0:T(8,128)(2,1)S(1)}, bf16[512,512]{1,0:T(8,128)(2,1)}, u32[]{:S(2)}) %copy-start) | copy-done | bytes 524312
  78.6 0.0 copy-start.1
  78.6 0.9 %copy-done.1 = f32[2,64,512]{2,1,0:T(8,128)S(1)} copy-done((f32[2,64,512]{2,1,0:T(8,128)S(1)}, f32[2,64,512]{2,1,0:T(8,128)}, u32[]{:S(2)}) %copy-start.1) | copy-done | bytes 262168
  79.6 0.0 copy-start.2
  79.6 0.9 %copy-done.2 = f32[2,8,2048]{2,1,0:T(8,128)S(1)} copy-done((f32[2,8,2048]{2,1,0:T(8,128)S(1)}, f32[2,8,2048]{2,1,0:T(8,128)}, u32[]{:S(2)}) %copy-start.2) | copy-done | bytes 131096
  80.5 1.0 %finish.1 = (bf16[512,512]{1,0:T(8,128)(2,1)}, f32[2,64,512]{2,1,0:T(8,128)}, f32[8,2,2048]{2,1,0:T(2,128)}) custom-call(bf16[512,512]{1,0:T(8,128)(2,1)S(1)} %copy-done, f32[2,64,512]{2,1,0:T(8,128)S(1)} %copy-done.1, f32[2,8,2048]{2,1,0:T(8,128)S(1)} %copy-done.2), custom_call_target="tpu_custom_call" | custom-call | tf_op jit(solution)/shard_map/finish/pallas_call | solution.py:625
Async XLA Ops:
  77.6 1.0 %copy-start = (bf16[512,512]{1,0:T(8,128)(2,1)S(1)}, bf16[512,512]{1,0:T(8,128)(2,1)}, u32[]{:S(2)}) copy-start(bf16[512,512]{1,0:T(8,128)(2,1)} %get-tuple-element.9.gh) | copy-start | bytes 1572868
  78.6 0.9 %copy-start.1 = (f32[2,64,512]{2,1,0:T(8,128)S(1)}, f32[2,64,512]{2,1,0:T(8,128)}, u32[]{:S(2)}) copy-start(f32[2,64,512]{2,1,0:T(8,128)} %get-tuple-element.10.gi) | copy-start | bytes 786436
  79.6 0.9 %copy-start.2 = (f32[2,8,2048]{2,1,0:T(8,128)S(1)}, f32[2,8,2048]{2,1,0:T(8,128)}, u32[]{:S(2)}) copy-start(f32[2,8,2048]{2,1,0:T(8,128)} %get-tuple-element.11.go) | copy-start | bytes 393220

commit v6 on v5

--- a/solution.py
+++ b/solution.py
@@ -271,7 +271,7 @@
         logits[:, cols] = jnp.dot(normed[...], head, preferred_element_type=F32)
     dr_col[...] = jnp.broadcast_to(target.astype(F32), (128, 128))
 
-    @pl.loop(0, 8, unroll=2)
+    @pl.loop(0, 8, unroll=4)
     def soft(i):
         rows = pl.ds(pl.multiple_of(i * 16, 16), 16)
         value = logits[rows, :]
@@ -289,7 +289,7 @@
             d_logit[...], head, NT, preferred_element_type=F32
         )
 
-    @pl.loop(0, 8, unroll=4)
+    @pl.loop(0, 8, unroll=8)
     def unnorm(i):
         rows = pl.ds(pl.multiple_of(i * 16, 16), 16)
         value, scale = x_rows[rows, :], scale_col[rows, :1]
@@ -470,7 +470,6 @@
     for s in range(2):
         ip_x[s] = in_block(0, s).astype(BF)
     ip_beside = post.send(ip_x, ip_xg, beside)
-    grad_in_piece(5)
     for copy in gb_ys:
         copy.wait_recv()
     value = gb_sum[y].astype(F32)
@@ -478,13 +477,17 @@
         value = value + gb_yg[i].astype(F32)
     gp_z[...] = value.astype(BF)
     gp_across = post.send(gp_z, gp_zg, zs[2])
+    grad_in_piece(5)
     grad_in_piece(6)
     for copy in ga_xs:
         copy.wait_recv()
     value = ga_sum[x_lo, x_hi].astype(F32)
     for i in range(3):
         value = value + ga_xg[i].astype(F32)
-    gp_rows[...] = value
+    gp_across.wait_recv()
+    gp_rows[...] = value + gp_zg[...].astype(F32)
+    theirs = gp_rows.at[pl.ds(pl.multiple_of((1 - step) * 8, 8), 8), :]
+    gp_swap_rows = post.send(theirs, gp_pair, pair)
     grad_in_piece(7)
 
     ratio_row = ratio_rows[0:1, :]
@@ -509,10 +512,6 @@
 
     back(0)
     back(1)
-    gp_across.wait_recv()
-    gp_rows[...] = gp_rows[...] + gp_zg[...].astype(F32)
-    theirs = gp_rows.at[pl.ds(pl.multiple_of((1 - step) * 8, 8), 8), :]
-    gp_swap_rows = post.send(theirs, gp_pair, pair)
     back(2)
     back(3)
     ip_beside.wait_recv()
@@ -631,7 +630,6 @@
         ],
         in_specs=[vmem] * 3,
         out_specs=[vmem] * 3,
-        compiler_params=pltpu.CompilerParams(vmem_limit_bytes=4 * 1024 * 1024),
         name="finish",
     )(grad_hidden, grad_in, grad_out)
     return grad_hidden, jnp.transpose(grad_in, (0, 2, 1)), grad_out

time: 81.7 us -> 78.5 us (0.961); the launches traced: 81.5 us -> 77.4 us
  local copies, waits for them, and re-layouts: 2.89 us -> 0 us
  Pallas kernels: 77.9 us -> 76.8 us
    unnamed x6 -> x0, local copies, waits for them, and re-layouts: 2.89 us -> none
    pallas_call x1, Pallas kernels: 77 us -> 74.7 us  [shards(): pl.pallas_call(functools.partial(kernel, loss_weight, width_in), out_shap...]
    pallas_call x1, Pallas kernels: 0.97 us -> 2.07 us  [shards(): pl.pallas_call(finish, out_shape=[jax.ShapeDtypeStruct((frames, units), B...]
where the time goes in v6:
time: 78.5 us; the launch traced here: 77.4 us
  Pallas kernels  76.8 us (98%)
    pallas_call x1, Pallas kernels, shards(): pl.pallas_call(functools.partial(kernel, loss_weight, width_in), out_shap...  74.7 us
    pallas_call x1, Pallas kernels, shards(): pl.pallas_call(finish, out_shape=[jax.ShapeDtypeStruct((frames, units), B...  2.07 us

profile of v6, /device:TPU:0, one launch (start us, length us, event | category | flops | bytes accessed | tf_op | source)
XLA Modules:
  0.0 77.4 jit_solution(14017598946676432421)
XLA Ops:
  0.6 74.7 %whole.1 = (bf16[512,512]{1,0:T(8,128)(2,1)}, f32[2,64,512]{2,1,0:T(8,128)}, f32[2,8,2048]{2,1,0:T(8,128)}) custom-call(bf16[512,512]{1,0:T(8,128)(2,1)} %hidden_in.1, bf16[2,512,1024]{2,1,0:T(8,128)(2,1)} %w_in_in.1, bf16[2048,1024]{1,0:T(8,128)(2,1)} %bitcast.2, f32[2,1024]{1,0:T(2,128)} %gain_in.1, bf16[8,2,2048]{2,1,0:T(2,128)(2,1)} %w_out.1, s32[2,64]{1,0:T(2,128)} %ids.1), custom_call_target="tpu_custom_call" | custom-call | tf_op jit(solution)/shard_map/whole/pallas_call | solution.py:604
  75.3 2.1 %finish.1 = (bf16[512,512]{1,0:T(8,128)(2,1)}, f32[2,64,512]{2,1,0:T(8,128)}, f32[8,2,2048]{2,1,0:T(2,128)}) custom-call(bf16[512,512]{1,0:T(8,128)(2,1)} %get-tuple-element.9.gh, f32[2,64,512]{2,1,0:T(8,128)} %get-tuple-element.10.gi, f32[2,8,2048]{2,1,0:T(8,128)} %get-tuple-element.11.go), custom_call_target="tpu_custom_call" | custom-call | tf_op jit(solution)/shard_map/finish/pallas_call | solution.py:624

commit v7 on v6

--- a/solution.py
+++ b/solution.py
@@ -394,11 +394,13 @@
 
     ip_ys, ip_relay = [[], []], [[], []]
 
-    def grad_in_piece(k):
+    swaps = {}
+
+    def grad_in_product(k):
         for copy in d_z_copies[k]:
             copy.wait_recv()
         b, to_y = piece(k)
-        late, i = k // 4, k % 4
+        late = k // 4
         rows = [d_all[s, b, to_y] for s in range(2)]
         product = jnp.dot(
             jnp.concatenate(rows, axis=0), scaled[...], preferred_element_type=F32
@@ -407,8 +409,12 @@
             for e in range(2):
                 start = s * 128 + e * 64
                 ip[late, to_y, e, s] = product[start : start + 64]
-        swap = post.send(ip.at[late, to_y, 1 - c], ip_c.at[late, to_y], twin)
-        swap.wait_recv()
+        swaps[k] = post.send(ip.at[late, to_y, 1 - c], ip_c.at[late, to_y], twin)
+
+    def grad_in_sum(k):
+        b, to_y = piece(k)
+        late, i = k // 4, k % 4
+        swaps[k].wait_recv()
         if i == 3:
             return
         if i:
@@ -426,6 +432,10 @@
             for s, d in ((0, 1), (1, 3)):
                 ip_relay[late].append(post.send(ip_y.at[late, 0, s], ip_rel.at[late, s], ys[d]))
 
+    def grad_in_piece(k):
+        grad_in_product(k)
+        grad_in_sum(k)
+
     def in_block(late, s):
         value = ip[late, y, c, s].astype(F32) + ip_c[late, y, s].astype(F32)
         for i in range(2):
@@ -477,8 +487,9 @@
         value = value + gb_yg[i].astype(F32)
     gp_z[...] = value.astype(BF)
     gp_across = post.send(gp_z, gp_zg, zs[2])
-    grad_in_piece(5)
-    grad_in_piece(6)
+    grad_in_product(5)
+    grad_in_product(6)
+    grad_in_sum(5)
     for copy in ga_xs:
         copy.wait_recv()
     value = ga_sum[x_lo, x_hi].astype(F32)
@@ -488,7 +499,8 @@
     gp_rows[...] = value + gp_zg[...].astype(F32)
     theirs = gp_rows.at[pl.ds(pl.multiple_of((1 - step) * 8, 8), 8), :]
     gp_swap_rows = post.send(theirs, gp_pair, pair)
-    grad_in_piece(7)
+    grad_in_product(7)
+    grad_in_sum(6)
 
     ratio_row = ratio_rows[0:1, :]
     for copy in small_copies:
@@ -515,6 +527,7 @@
     back(2)
     back(3)
     ip_beside.wait_recv()
+    grad_in_sum(7)
     for copy in ip_ys[1]:
         copy.wait_recv()
     for s in range(2):

time: 78.5 us -> 78.5 us (level)
  no operation moved by 1% of the time
where the time goes in v7:
time: 78.5 us; the launch traced here: 77.4 us
  Pallas kernels  76.8 us (98%)
    pallas_call x1, Pallas kernels, shards(): pl.pallas_call(functools.partial(kernel, loss_weight, width_in), out_shap...  74.7 us
    pallas_call x1, Pallas kernels, shards(): pl.pallas_call(finish, out_shape=[jax.ShapeDtypeStruct((frames, units), B...  2.07 us

profile of v7, /device:TPU:0, one launch (start us, length us, event | category | flops | bytes accessed | tf_op | source)
XLA Modules:
  0.0 77.4 jit_solution(11391082493751079426)
XLA Ops:
  0.6 74.7 %whole.1 = (bf16[512,512]{1,0:T(8,128)(2,1)}, f32[2,64,512]{2,1,0:T(8,128)}, f32[2,8,2048]{2,1,0:T(8,128)}) custom-call(bf16[512,512]{1,0:T(8,128)(2,1)} %hidden_in.1, bf16[2,512,1024]{2,1,0:T(8,128)(2,1)} %w_in_in.1, bf16[2048,1024]{1,0:T(8,128)(2,1)} %bitcast.2, f32[2,1024]{1,0:T(2,128)} %gain_in.1, bf16[8,2,2048]{2,1,0:T(2,128)(2,1)} %w_out.1, s32[2,64]{1,0:T(2,128)} %ids.1), custom_call_target="tpu_custom_call" | custom-call | tf_op jit(solution)/shard_map/whole/pallas_call | solution.py:617
  75.3 2.1 %finish.1 = (bf16[512,512]{1,0:T(8,128)(2,1)}, f32[2,64,512]{2,1,0:T(8,128)}, f32[8,2,2048]{2,1,0:T(2,128)}) custom-call(bf16[512,512]{1,0:T(8,128)(2,1)} %get-tuple-element.9.gh, f32[2,64,512]{2,1,0:T(8,128)} %get-tuple-element.10.gi, f32[2,8,2048]{2,1,0:T(8,128)} %get-tuple-element.11.go), custom_call_target="tpu_custom_call" | custom-call | tf_op jit(solution)/shard_map/finish/pallas_call | solution.py:637

commit v8 on v6

--- a/solution.py
+++ b/solution.py
@@ -307,10 +307,24 @@
     def piece(k):
         return (1 - x_lo if k < 4 else x_lo), lax.rem(y + order[k % 4], 4)
 
-    d_x_copies, d_z_copies = [], [[] for _ in range(8)]
-    for k in range(8):
+    d_x_copies, d_z_copies = {}, [[] for _ in range(8)]
+    for k in (0, 1, 2, 4, 5, 6, 7):
         b, to_y = piece(k)
-        d_x_copies.append(post.send(d_turn.at[b, to_y], d_all.at[step, b, to_y, :, lane], far))
+        d_x_copies[k] = post.send(d_turn.at[b, to_y], d_all.at[step, b, to_y, :, lane], far)
+
+    def send_across():
+        b, to_y = piece(3)
+        for copy in d_z_copies[3]:
+            copy.wait_recv()
+        d_z_copies[3] = [
+            post.send(d_turn.at[b, to_y], d_all.at[step, b, to_y, :, lane], far)
+        ]
+        for dz in (1, 2, 3):
+            to_z = lax.rem(z + dz, 4)
+            view = d_all.at[
+                lax.rem(to_z, 2), b, to_y, :, at128(x_hi * 2 + lax.div(to_z, 2))
+            ]
+            d_z_copies[3].append(post.send(view, view, far))
 
     def send_own(k):
         b, to_y = piece(k)
@@ -384,7 +398,8 @@
         post.send(gb_part(2, 0), gb_xg.at[1, 0], xs[3]),
     ]
     for k in range(8):
-        send_far(k)
+        if k != 3:
+            send_far(k)
         if k < 5:
             send_own(k + 3)
     ga_relay[0].wait_recv()
@@ -437,6 +452,7 @@
     gb_xs.append(post.send(gb_part(1, 0, 0), gb_xg.at[0, 0], xs[1]))
     gb_relay[1].wait_recv()
     gb_xs.append(post.send(gb_part(2, 1, 1), gb_xg.at[1, 1], xs[3]))
+    send_across()
     grad_in_piece(1)
     grad_in_piece(2)
     for copy in ga_ys:

time: 78.5 us -> 77.8 us (level)
  no operation moved by 1% of the time
where the time goes in v8:
time: 77.8 us; the launch traced here: 77 us
  Pallas kernels  76.3 us (98%)
    pallas_call x1, Pallas kernels, shards(): pl.pallas_call(functools.partial(kernel, loss_weight, width_in), out_shap...  74.3 us
    pallas_call x1, Pallas kernels, shards(): pl.pallas_call(finish, out_shape=[jax.ShapeDtypeStruct((frames, units), B...  2.07 us

profile of v8, /device:TPU:0, one launch (start us, length us, event | category | flops | bytes accessed | tf_op | source)
XLA Modules:
  0.0 77.0 jit_solution(16669151905896452654)
XLA Ops:
  0.6 74.3 %whole.1 = (bf16[512,512]{1,0:T(8,128)(2,1)}, f32[2,64,512]{2,1,0:T(8,128)}, f32[2,8,2048]{2,1,0:T(8,128)}) custom-call(bf16[512,512]{1,0:T(8,128)(2,1)} %hidden_in.1, bf16[2,512,1024]{2,1,0:T(8,128)(2,1)} %w_in_in.1, bf16[2048,1024]{1,0:T(8,128)(2,1)} %bitcast.2, f32[2,1024]{1,0:T(2,128)} %gain_in.1, bf16[8,2,2048]{2,1,0:T(2,128)(2,1)} %w_out.1, s32[2,64]{1,0:T(2,128)} %ids.1), custom_call_target="tpu_custom_call" | custom-call | tf_op jit(solution)/shard_map/whole/pallas_call | solution.py:620
  74.9 2.1 %finish.1 = (bf16[512,512]{1,0:T(8,128)(2,1)}, f32[2,64,512]{2,1,0:T(8,128)}, f32[8,2,2048]{2,1,0:T(2,128)}) custom-call(bf16[512,512]{1,0:T(8,128)(2,1)} %get-tuple-element.9.gh, f32[2,64,512]{2,1,0:T(8,128)} %get-tuple-element.10.gi, f32[2,8,2048]{2,1,0:T(8,128)} %get-tuple-element.11.go), custom_call_target="tpu_custom_call" | custom-call | tf_op jit(solution)/shard_map/finish/pallas_call | solution.py:640

commit v9 on v8

--- a/solution.py
+++ b/solution.py
@@ -308,15 +308,15 @@
         return (1 - x_lo if k < 4 else x_lo), lax.rem(y + order[k % 4], 4)
 
     d_x_copies, d_z_copies = {}, [[] for _ in range(8)]
-    for k in (0, 1, 2, 4, 5, 6, 7):
+    for k in (0, 1, 2, 4, 5, 6):
         b, to_y = piece(k)
         d_x_copies[k] = post.send(d_turn.at[b, to_y], d_all.at[step, b, to_y, :, lane], far)
 
-    def send_across():
-        b, to_y = piece(3)
-        for copy in d_z_copies[3]:
+    def send_across(k):
+        b, to_y = piece(k)
+        for copy in d_z_copies[k]:
             copy.wait_recv()
-        d_z_copies[3] = [
+        d_z_copies[k] = [
             post.send(d_turn.at[b, to_y], d_all.at[step, b, to_y, :, lane], far)
         ]
         for dz in (1, 2, 3):
@@ -324,7 +324,7 @@
             view = d_all.at[
                 lax.rem(to_z, 2), b, to_y, :, at128(x_hi * 2 + lax.div(to_z, 2))
             ]
-            d_z_copies[3].append(post.send(view, view, far))
+            d_z_copies[k].append(post.send(view, view, far))
 
     def send_own(k):
         b, to_y = piece(k)
@@ -398,7 +398,7 @@
         post.send(gb_part(2, 0), gb_xg.at[1, 0], xs[3]),
     ]
     for k in range(8):
-        if k != 3:
+        if k % 4 != 3:
             send_far(k)
         if k < 5:
             send_own(k + 3)
@@ -452,7 +452,7 @@
     gb_xs.append(post.send(gb_part(1, 0, 0), gb_xg.at[0, 0], xs[1]))
     gb_relay[1].wait_recv()
     gb_xs.append(post.send(gb_part(2, 1, 1), gb_xg.at[1, 1], xs[3]))
-    send_across()
+    send_across(3)
     grad_in_piece(1)
     grad_in_piece(2)
     for copy in ga_ys:
@@ -480,6 +480,7 @@
     for i, d in enumerate(order[:3]):
         gb_ys.append(post.send(gb_sum.at[lax.rem(y + d, 4)], gb_yg.at[i], ys[d]))
     grad_in_piece(3)
+    send_across(7)
     grad_in_piece(4)
     for copy in ip_ys[0]:
         copy.wait_recv()

time: 77.8 us -> 79.2 us (1.018)
  Pallas kernels: 76.3 us -> 77.1 us
where the time goes in v9:
time: 79.2 us; the launch traced here: 77.7 us
  Pallas kernels  77.1 us (97%)
    pallas_call x1, Pallas kernels, shards(): pl.pallas_call(functools.partial(kernel, loss_weight, width_in), out_shap...  75 us
    pallas_call x1, Pallas kernels, shards(): pl.pallas_call(finish, out_shape=[jax.ShapeDtypeStruct((frames, units), B...  2.07 us

profile of v9, /device:TPU:0, one launch (start us, length us, event | category | flops | bytes accessed | tf_op | source)
XLA Modules:
  0.0 77.7 jit_solution(18338313192049952658)
XLA Ops:
  0.6 75.0 %whole.1 = (bf16[512,512]{1,0:T(8,128)(2,1)}, f32[2,64,512]{2,1,0:T(8,128)}, f32[2,8,2048]{2,1,0:T(8,128)}) custom-call(bf16[512,512]{1,0:T(8,128)(2,1)} %hidden_in.1, bf16[2,512,1024]{2,1,0:T(8,128)(2,1)} %w_in_in.1, bf16[2048,1024]{1,0:T(8,128)(2,1)} %bitcast.2, f32[2,1024]{1,0:T(2,128)} %gain_in.1, bf16[8,2,2048]{2,1,0:T(2,128)(2,1)} %w_out.1, s32[2,64]{1,0:T(2,128)} %ids.1), custom_call_target="tpu_custom_call" | custom-call | tf_op jit(solution)/shard_map/whole/pallas_call | solution.py:621
  75.6 2.1 %finish.1 = (bf16[512,512]{1,0:T(8,128)(2,1)}, f32[2,64,512]{2,1,0:T(8,128)}, f32[8,2,2048]{2,1,0:T(2,128)}) custom-call(bf16[512,512]{1,0:T(8,128)(2,1)} %get-tuple-element.9.gh, f32[2,64,512]{2,1,0:T(8,128)} %get-tuple-element.10.gi, f32[2,8,2048]{2,1,0:T(8,128)} %get-tuple-element.11.go), custom_call_target="tpu_custom_call" | custom-call | tf_op jit(solution)/shard_map/finish/pallas_call | solution.py:641
